TPU v7x, 1024 devices: a whole 8x8x8 slice. The times are simulated.
1024 devices in a mesh: dp: 16 (over z, core), seq: 64 (over x, y).
Axes of the slice: x: 8, y: 8, z: 8, core: 2. Of those that a mesh axis runs over, the one named last changes fastest.
Arguments:
- patches: bfloat16 [196608, 1280], P(('dp', 'seq')), may hold values from -6 to 6
- query_key_value: bfloat16 [196608, 3840], P(('dp', 'seq')), may hold values from -100 to 100
- counts: int32 [1024, 4], P(('dp', 'seq')), may hold values from 4 to 48, as said below
- owner_index: int32 [49152, 1], P(('dp', 'seq')), may hold values from 0 to 63; in each aligned block of 48 rows (0 to 47, 48 to 95, ...) at most 2 rows name the same one
- out_weight: bfloat16 [1280, 1280], P(None, 'dp'), may hold values from -0.15625 to 0.15625
- ln_gain: float32 [1280], replicated, may hold values from 0.25 to 1.75
- ln_bias: float32 [1280], replicated, may hold values from -3 to 3
Outputs:
- image_tokens: bfloat16 [131072, 5120], P(('dp', 'seq'))
Inputs may be any that keep to these rules, and one draw needn't show every extreme that they name: Every count is a multiple of 4, each device's counts sum to at most 192, and some device's counts sum to exactly 192. `owner_index`: among the merge groups of one device, at most 2 name the same owner.
All inputs are finite; a program needn't handle non-finite values.
Results may differ from a plain program's by a relative error of at most 0.0029.
Values may be sent and summed in bfloat16 or wider, within the bound.
No kernel may reach another device: no remote copies, remote signals or barrier semaphores. Data moves between devices by JAX's collectives and lax.ppermute only.
A program may use at most 32 MiB of HBM per device.

v0:
```python
import jax
import jax.numpy as jnp
from jax import lax
from jax.sharding import PartitionSpec as P

HEADS = 16
IMGS = 4


def segment_rows(count_row, row_count):
    image_ends = jnp.cumsum(count_row)
    row_ids = jnp.arange(row_count, dtype=jnp.int32)
    return jnp.sum((row_ids[:, None] >= image_ends[None, :]).astype(jnp.int32), axis=1)


def attend(packed, segment_ids, model_width):
    row_count = packed.shape[0]
    head_size = model_width // HEADS
    queries = packed[:, :model_width].reshape(row_count, HEADS, head_size)
    keys_all = packed[:, model_width : 2 * model_width].reshape(row_count, HEADS, head_size)
    values_all = packed[:, 2 * model_width :].reshape(row_count, HEADS, head_size)
    scores = jnp.einsum(
        "qhd,khd->hqk", queries, keys_all, preferred_element_type=jnp.float32
    ) * head_size ** (-0.5)
    same_image = segment_ids[:, None] == segment_ids[None, :]
    scores = jnp.where(same_image[None, :, :], scores, -1e30)
    top_score = jnp.max(scores, axis=2, keepdims=True)
    expo = jnp.exp(scores - top_score)
    attn_weights = (expo / jnp.sum(expo, axis=2, keepdims=True)).astype(jnp.bfloat16)
    context = jnp.einsum(
        "hqk,khd->qhd", attn_weights, values_all, preferred_element_type=jnp.float32
    )
    return context.reshape(row_count, model_width).astype(jnp.bfloat16)


def merge_and_place(hidden, segment_ids, owners, ln_gain, ln_bias, owner_count, capacity):
    row_count, model_width = hidden.shape
    row_mean = jnp.mean(hidden, axis=1, keepdims=True)
    centered = hidden - row_mean
    row_var = jnp.mean(centered * centered, axis=1, keepdims=True)
    normed = (centered * lax.rsqrt(row_var + 1e-06) * ln_gain[None, :] + ln_bias[None, :]).astype(
        jnp.bfloat16
    )
    merged = normed.reshape(row_count // 4, 4 * model_width)
    live_group = segment_ids.reshape(row_count // 4, 4)[:, 0] < IMGS
    group_ids = jnp.arange(row_count // 4, dtype=jnp.int32)
    earlier = (
        (owners[None, :] == owners[:, None])
        & (group_ids[None, :] < group_ids[:, None])
        & live_group[None, :]
    )
    slot_index = jnp.sum(earlier.astype(jnp.int32), axis=1)
    target = owners * capacity + slot_index
    slot_ids = jnp.arange(owner_count * capacity, dtype=jnp.int32)
    onehot_map = ((slot_ids[:, None] == target[None, :]) & live_group[None, :]).astype(jnp.bfloat16)
    return jnp.dot(onehot_map, merged, preferred_element_type=jnp.float32).astype(jnp.bfloat16)


def body(patches, query_key_value, counts, owner_index, out_weight, ln_gain, ln_bias):
    row_count, model_width = patches.shape
    owner_count = lax.axis_size("seq")
    group_count = row_count // 4
    capacity = max(2, (group_count + owner_count - 1) // owner_count)
    segment_ids = segment_rows(counts[0], row_count)
    context = attend(query_key_value, segment_ids, model_width)
    projected = jnp.dot(
        context,
        lax.all_gather(out_weight, "dp", axis=1, tiled=True),
        preferred_element_type=jnp.float32,
    )
    hidden = patches.astype(jnp.float32) + projected
    outgoing = merge_and_place(
        hidden, segment_ids, owner_index[:, 0], ln_gain, ln_bias, owner_count, capacity
    )
    outgoing = outgoing.reshape(owner_count, capacity, 4 * model_width)
    received = lax.all_to_all(outgoing, "seq", split_axis=0, concat_axis=0, tiled=True)
    return received.reshape(owner_count * capacity, 4 * model_width)


def solution(mesh):
    placed = (
        P(("dp", "seq"), None),
        P(("dp", "seq"), None),
        P(("dp", "seq"), None),
        P(("dp", "seq"), None),
        P(None, "dp"),
        P(),
        P(),
    )
    return jax.shard_map(
        body, mesh=mesh, in_specs=placed, out_specs=P(("dp", "seq"), None), check_vma=False
    )
```

profile of v0, /device:TPU:4, one launch (start us, length us, event | category | flops | bytes accessed | tf_op | source)
XLA Modules:
  0.0 131.5 jit_solution(11283096986864556076)
XLA Ops:
  6.5 0.0 all-gather.2.cloned.1.call-start
  6.5 0.7 all-gather.2.cloned.1.call-update
  7.3 0.0 copy-start.4
  7.3 0.0 copy-start.2
  7.3 1.4 %fusion.18 = (bf16[192,1280]{1,0:T(8,128)(2,1)S(1)}, bf16[192,1280]{1,0:T(8,128)(2,1)S(1)}, bf16[192,1280]{1,0:T(8,128)(2,1)S(1)}) fusion(bf16[192,3840]{1,0:T(8,128)(2,1)} %param.8), kind=kLoop, calls=%fused_computation.33 | loop fusion | bytes 2949120 | tf_op jit(solution)/shard_map/slice | solution.py:20
  8.7 0.2 copy.20
  9.0 0.2 copy.21
  9.2 0.2 copy.22
  9.4 0.0 copy-done.4
  9.4 0.2 reduce-window.8
  9.6 0.1 convert_reduce_fusion.1
  9.7 0.1 reshape.108
  9.8 0.1 fusion.15
  9.9 0.0 copy-done.2
  9.9 0.2 convert_reduce_fusion
  10.1 0.1 broadcast_compare_fusion
  10.2 3.0 %fusion.19 = (f32[16,192]{1,0:T(8,128)S(1)}, f32[16,192,192]{1,2,0:T(8,128)}) fusion(pred[192,192]{0,1:T(8,128)(4,1)S(1)} %broadcast_compare_fusion, bf16[192,16,80]{0,2,1:T(8,128)(2,1)S(1)} %bitcast.18, bf16[192,16,80]{0,2,1:T(8,128)(2,1)S(1)} %bitcast.20), kind=kOutput, calls=%fused_computation.34 | convolution fusion | flops 96731328 | bytes 3391488 | tf_op jit(solution)/shard_map/sub | solution.py:28
  13.2 0.0 copy-start.3
  13.2 2.4 %fusion.6 = bf16[16,192,80]{1,2,0:T(8,128)(2,1)S(1)} fusion(bf16[192,16,80]{0,2,1:T(8,128)(2,1)S(1)} %bitcast.19, f32[16,192,192]{1,2,0:T(8,128)} %get-tuple-element.9, f32[16,192]{1,0:T(8,128)S(1)} %get-tuple-element.8), kind=kOutput, calls=%fused_computation.11 | convolution fusion | flops 95797248 | bytes 3354624 | tf_op jit(solution)/shard_map/hqk,khd->qhd/dot_general | solution.py:30
  15.6 53.9 %all-gather.2.cloned.1.call-done = bf16[1280,1280]{0,1:T(8,128)(2,1)} async-done(((bf16[1280,80]{0,1:T(8,128)(2,1)}), bf16[1280,1280]{0,1:T(8,128)(2,1)}) %all-gather.2.cloned.1.call-update) | async-done | bytes 3276816 | tf_op jit(solution)/shard_map/all_gather | solution.py:68
  69.4 0.0 copy-done.3
  69.5 0.0 copy-start
  69.5 3.3 %fusion.20 = (f32[192]{0:T(256)S(1)}, f32[192,1280]{1,0:T(8,128)S(1)}) fusion(bf16[192,1280]{0,1:T(8,128)(2,1)S(1)} %bitcast.23, bf16[1280,1280]{0,1:T(8,128)(2,1)} %all-gather.2.cloned.1.call-done, bf16[192,1280]{1,0:T(8,128)(2,1)S(1)} %copy-done.3), kind=kOutput, calls=%fused_computation.35 | convolution fusion | flops 629882688 | bytes 5243648 | tf_op jit(solution)/shard_map/dot_general | solution.py:66
  72.8 0.2 multiply_reduce_fusion
  73.0 0.0 copy-done
  73.0 0.0 copy-done.1
  73.0 0.2 add_convert_fusion
  73.3 0.3 reshape.112
  73.6 0.5 convolution_convert_fusion
  74.1 0.5 reshape.113
  74.6 48.7 %all_to_all.5 = bf16[64,2,5120]{2,1,0:T(2,128)(2,1)S(1)} all-to-all(bf16[64,2,5120]{2,1,0:T(2,128)(2,1)S(1)} %reshape.113), channel_id=1, replica_groups=mesh['dp'=16,'seq'=64] {'seq'}, dimensions={0} | all-to-all | bytes 2621440 | tf_op jit(solution)/shard_map/all_to_all | solution.py:76
  123.3 1.3 %reshape.114 = bf16[128,5120]{1,0:T(8,128)(2,1)} reshape(bf16[64,2,5120]{2,1,0:T(2,128)(2,1)S(1)} %all_to_all.5) | data formatting | bytes 2621440 | tf_op jit(solution)/shard_map/reshape | solution.py:77
  (4 shorter events, 0.0 us)
Async XLA Ops:
  6.5 62.9 %all-gather.2.cloned.1.call-start = ((), (), s32[]{:S(2)}) async-start(), calls=%async_computation.1 | async-start | bytes 3481600 | tf_op jit(solution)/shard_map/all_gather | solution.py:68
  7.3 2.2 %copy-start.4 = (s32[1,4]{1,0:T(1,128)S(1)}, s32[1,4]{1,0:T(1,128)}, u32[]{:S(2)}) copy-start(s32[1,4]{1,0:T(1,128)} %param.9) | copy-start | bytes 52
  7.3 2.7 %copy-start.2 = (s32[48,1]{0,1:T(1,128)S(1)}, s32[48,1]{0,1:T(1,128)}, u32[]{:S(2)}) copy-start(s32[48,1]{0,1:T(1,128)} %param.10) | copy-start | bytes 580
  13.2 56.2 %copy-start.3 = (bf16[192,1280]{1,0:T(8,128)(2,1)S(1)}, bf16[192,1280]{1,0:T(8,128)(2,1)}, u32[]{:S(2)}) copy-start(bf16[192,1280]{1,0:T(8,128)(2,1)} %param.7) | copy-start | bytes 1474564
  69.5 3.6 %copy-start = (f32[1280]{0:T(1024)S(1)}, f32[1280]{0:T(1024)}, u32[]{:S(2)}) copy-start(f32[1280]{0:T(1024)} %param.13) | copy-start | bytes 15364
  69.5 3.6 %copy-start.1 = (f32[1280]{0:T(1024)S(1)}, f32[1280]{0:T(1024)}, u32[]{:S(2)}) copy-start(f32[1280]{0:T(1024)} %param.12) | copy-start | bytes 15364
Sparse Core Ops, SparseCore 0:
  10.0 59.3 all-gather.1
where the time goes:
time: 132 us; the launch traced here: 131 us
  waiting for transfers between devices  54.6 us (41%)
  blocking collectives  48.7 us (37%)
  between operations  13.5 us (10%)
  matrix products  9.11 us (7%)
  local copies, waits for them, and re-layouts  4.45 us (3%)
    all_gather x1, waiting for transfers between devices, body(): lax.all_gather(out_weight, 'dp', axis=1, tiled=True)  53.9 us
    all_to_all x1, blocking collectives, body(): lax.all_to_all(outgoing, 'seq', split_axis=0, concat_axis=0, tiled=True)  48.7 us
    dot_general x1, matrix products, body(): jnp.dot(context, lax.all_gather(out_weight, 'dp', axis=1, tiled=True), pr...  3.3 us
    sub x1, matrix products, attend(): expo = jnp.exp(scores - top_score)  2.97 us
  transfers between devices with their start and end apart: 1, of which 1 were waited for; matrix products, arithmetic and copies ran while one was open for 6% of the time, Pallas kernels for 0%

commit v1 on v0

v1 whole, which is shorter than its diff:
```python
import functools

import jax
import jax.numpy as jnp
from jax import lax
from jax.experimental import pallas as pl
from jax.experimental.pallas import tpu as pltpu
from jax.sharding import PartitionSpec as P


HEADS = 16
IMGS = 4
DEAD = -1000
VMEM = pl.BlockSpec(memory_space=pltpu.VMEM)
SMEM = pl.BlockSpec(memory_space=pltpu.SMEM)
HBM = pl.BlockSpec(memory_space=pltpu.HBM)
F32 = jnp.float32
BF16 = jnp.bfloat16


def iota(shape, dim):
    return lax.broadcasted_iota(jnp.int32, shape, dim)


def pick(hits, values):
    return lax.dot_general(
        jnp.where(hits, 1.0, 0.0).astype(BF16), values, (((1,), (0,)), ((), ())), preferred_element_type=F32
    )


def call(kernel, out_shape, operands, flops, scratch=(), smem=0, limit=8, out_specs=VMEM):
    return pl.pallas_call(
        kernel,
        out_shape=out_shape,
        in_specs=[SMEM] * smem + [VMEM] * (len(operands) - smem),
        out_specs=out_specs,
        scratch_shapes=list(scratch),
        compiler_params=pltpu.CompilerParams(vmem_limit_bytes=limit * 1024 * 1024),
        cost_estimate=pl.CostEstimate(flops=flops, bytes_accessed=1 << 20, transcendentals=0),
    )(*operands)


def image_ends(counts_ref):
    ends, end = [], 0
    for image in range(IMGS):
        end = end + counts_ref[0, image]
        ends.append(end)
    return ends


def row_slots(ends, owner_row, owner_col):
    rows = owner_row.shape[1]
    lane, sub = iota((1, rows), 1), iota((rows, 1), 0)
    first = lane - (lane & 3)
    earlier = (owner_col == owner_row) & (sub < first) & ((sub & 3) == 0) & (sub < ends[-1])
    slot = jnp.sum(jnp.where(earlier, 1.0, 0.0), axis=0, keepdims=True)
    return slot, first < ends[-1], lane & 3


def front_kernel(
    counts_ref, owner_row_ref, owner_col_ref, packed_ref, patch_ref, context_out, send_ref, context_ref, done
):
    rows, width = patch_ref.shape
    head_size = width // HEADS
    ends = image_ends(counts_ref)
    lane, sub = iota((1, rows), 1), iota((rows, 1), 0)
    segment_row = sum((lane >= end).astype(jnp.int32) for end in ends)
    segment_col = sum((sub >= end).astype(jnp.int32) for end in ends)
    same_image = segment_col == segment_row
    for head in range(HEADS):
        low = head * head_size
        start = min(low // 128 * 128, width - 256)
        column = iota((1, 256), 1) + start
        mine = (column >= low) & (column < low + head_size)
        queries = packed_ref[:, start : start + 256]
        queries = jnp.where(mine, queries, jnp.zeros_like(queries))
        keys = packed_ref[:, width + start : width + start + 256]
        scores = lax.dot_general(
            queries, keys, (((1,), (1,)), ((), ())), preferred_element_type=F32
        ) * head_size ** (-0.5)
        scores = jnp.where(same_image, scores, -1e30)
        expo = jnp.exp(scores - jnp.max(scores, axis=1, keepdims=True))
        weights = (expo / jnp.sum(expo, axis=1, keepdims=True)).astype(BF16)
        values = packed_ref[:, 2 * width + start : 2 * width + start + 256]
        mixed = jnp.dot(weights, values, preferred_element_type=F32).astype(BF16)
        context_ref[:, start : start + 256] = jnp.where(mine, mixed, context_ref[:, start : start + 256])
    leave = pltpu.make_async_copy(context_ref, context_out, done)
    leave.start()
    slot, live, part = row_slots(ends, owner_row_ref[...], owner_col_ref[...])
    key = jnp.where(live & (slot == 0.0), owner_row_ref[...] * 8 + part, DEAD)
    line = iota((send_ref.shape[0], 1), 0)
    hits = key == line
    held = jnp.sum(jnp.where(hits, 1.0, 0.0), axis=1, keepdims=True)
    marker = jnp.where((held == 0.0) & ((line & 7) < 4), 64.0, 0.0)
    sent = pick(hits, patch_ref[...]) + pick(key == line - 4, context_ref[...]) + marker
    send_ref[...] = sent.astype(BF16)
    leave.wait()


def norm(hidden, gain, bias):
    gain, bias = gain[None, :], bias[None, :]
    inverse = 1.0 / hidden.shape[1]
    centered = hidden - jnp.sum(hidden, axis=1, keepdims=True) * inverse
    row_var = jnp.sum(centered * centered, axis=1, keepdims=True) * inverse
    return centered * lax.rsqrt(row_var + 1e-06) * gain + bias


def project(context, weight):
    return lax.dot_general(context, weight, (((1,), (1,)), ((), ())), preferred_element_type=F32)


def late_kernel(nz, splits, counts_ref, *refs):
    blocks, refs = refs[:nz], refs[nz:]
    halves, refs = refs[: len(splits)], refs[len(splits) :]
    owner_row_ref, owner_col_ref, context_ref, patch_ref, gain_ref, bias_ref = refs[:6]
    weight_out, send_ref, weight_ref, done = refs[6:]
    block_width = blocks[0].shape[0]
    me = lax.axis_index("dp")
    z, c = lax.shift_right_logical(me, 1), lax.bitwise_and(me, 1)

    def put(j, core, value):
        owner = lax.rem(z + j, nz) * 2 + core
        weight_ref[pl.ds(pl.multiple_of(owner * block_width, 16), block_width), :] = value

    for j in range(nz):
        put(j, c, blocks[j][...])
    for part, ref in zip(splits, halves):
        for i, j in enumerate(part):
            put(j, 1 - c, ref[i])
    leave = pltpu.make_async_copy(weight_ref, weight_out, done)
    leave.start()
    hidden = patch_ref[...].astype(F32) + project(context_ref[...], weight_ref[...])
    normed = norm(hidden, gain_ref[...], bias_ref[...]).astype(BF16)
    slot, live, part = row_slots(image_ends(counts_ref), owner_row_ref[...], owner_col_ref[...])
    key = jnp.where(live & (slot == 1.0), owner_row_ref[...] * 8 + 2 * part, DEAD)
    line = iota((send_ref.shape[0], 1), 0)
    half = send_ref.shape[1]
    sent = pick(key == line, normed[:, :half]) + pick(key == line - 1, normed[:, half:])
    send_ref[...] = sent.astype(BF16)
    leave.wait()


def early_kernel(received_ref, weight_ref, gain_ref, bias_ref, normed_ref):
    lines = received_ref.shape[0]
    owners = lines // 8
    row = iota((4 * owners, 1), 0)
    shift = owners.bit_length() - 1
    line = (row & (owners - 1)) * 8 + (row >> shift)
    column = iota((1, lines), 1)
    patches = pick(column == line, received_ref[...])
    context = pick(column == line + 4, received_ref[...]).astype(BF16)
    hidden = patches + project(context, weight_ref[...])
    normed = norm(hidden, gain_ref[...], bias_ref[...])
    normed_ref[...] = jnp.where(patches[:, :1] > 32.0, 0.0, normed).astype(BF16)


def join_kernel(normed_ref, received_ref, out_ref):
    lines, half = received_ref.shape
    owners = lines // 8
    row = iota((2 * owners, 1), 0)
    even = row == 2 * iota((1, owners), 1)
    column = iota((1, lines), 1)
    odd = (row & 1) == 1
    for part in range(4):
        for side in range(2):
            first = pick(even, normed_ref[part * owners : (part + 1) * owners, side * half : (side + 1) * half])
            hits = (column == 4 * (row - 1) + 2 * part + side) & odd
            start = (2 * part + side) * half
            out_ref[:, start : start + half] = (first + pick(hits, received_ref[...])).astype(BF16)


def pack_kernel(*refs):
    for i, ref in enumerate(refs[:-1]):
        refs[-1][i] = ref[...]


def pack(blocks):
    shape = jax.ShapeDtypeStruct((len(blocks), *blocks[0].shape), blocks[0].dtype)
    return call(pack_kernel, shape, blocks, 1 << 20, limit=1)


def ring_gather(shard):
    n_dp = lax.axis_size("dp")
    nz = n_dp // 2
    up = [(2 * z + c, 2 * ((z + 1) % nz) + c) for z in range(nz) for c in range(2)]
    down = [(2 * z + c, 2 * ((z - 1) % nz) + c) for z in range(nz) for c in range(2)]
    swap = [(d, d ^ 1) for d in range(n_dp)]
    blocks = [None] * nz
    blocks[0] = shard
    from_below, from_above = shard, shard
    for step in range(1, nz // 2 + 1):
        from_below = lax.ppermute(from_below, "dp", up)
        blocks[(-step) % nz] = from_below
        if step < nz - step:
            from_above = lax.ppermute(from_above, "dp", down)
            blocks[step] = from_above
    order = sorted(range(nz), key=lambda j: min(j, nz - j))
    splits = [s for s in (order[: nz // 2 + 1], order[nz // 2 + 1 :]) if s]
    halves = [lax.ppermute(pack([blocks[j] for j in part]), "dp", swap) for part in splits]
    return blocks, splits, halves


def step(patches, query_key_value, counts, owner_index, out_weight, ln_gain, ln_bias):
    rows, width = patches.shape
    owners = lax.axis_size("seq")
    nz = lax.axis_size("dp") // 2
    owner_col = jnp.repeat(owner_index, 4, axis=0)
    owner_row = owner_col.reshape(1, rows)

    blocks, splits, halves = ring_gather(out_weight.T)
    context, send = call(
      front_kernel,
      (pltpu.HBM((rows, width), BF16), jax.ShapeDtypeStruct((8 * owners, width), BF16)),
      [counts, owner_row, owner_col, query_key_value, patches],
      1 << 31,
      scratch=[pltpu.VMEM((rows, width), BF16), pltpu.SemaphoreType.DMA],
      smem=1,
      out_specs=(HBM, VMEM),
    )
    received = lax.all_to_all(send, "seq", split_axis=0, concat_axis=0, tiled=True)
    weight, late_send = call(
        functools.partial(late_kernel, nz, splits),
        (pltpu.HBM((width, width), BF16), jax.ShapeDtypeStruct((8 * owners, width // 2), BF16)),
        [counts, *blocks, *halves, owner_row, owner_col, context, patches, ln_gain, ln_bias],
        2 * rows * width * width,
        scratch=[pltpu.VMEM((width, width), BF16), pltpu.SemaphoreType.DMA],
        smem=1,
        out_specs=(HBM, VMEM),
    )
    late_received = lax.all_to_all(late_send, "seq", split_axis=0, concat_axis=0, tiled=True)
    normed = call(
        early_kernel,
        jax.ShapeDtypeStruct((4 * owners, width), BF16),
        [received, weight, ln_gain, ln_bias],
        8 * owners * width * width,
    )
    return call(join_kernel, jax.ShapeDtypeStruct((2 * owners, 4 * width), BF16), [normed, late_received], 1 << 29)


def solution(mesh):
    placed = (
        P(("dp", "seq"), None),
        P(("dp", "seq"), None),
        P(("dp", "seq"), None),
        P(("dp", "seq"), None),
        P(None, "dp"),
        P(),
        P(),
    )
    return jax.shard_map(step, mesh=mesh, in_specs=placed, out_specs=P(("dp", "seq"), None), check_vma=False)
```

time: 132 us -> 121 us (0.917)
  starting transfers between devices: 0.01 us -> 65.6 us
  blocking collectives: 48.7 us -> 0 us
  waiting for transfers between devices: 54.6 us -> 33.1 us
  Pallas kernels: 0 us -> 15.1 us
  between operations: 13.5 us -> 0.27 us
  matrix products: 9.11 us -> 0 us
  local copies, waits for them, and re-layouts: 4.45 us -> 5.92 us
    all_gather x1 -> x0, waiting for transfers between devices: 53.9 us -> none  [body(): lax.all_gather(out_weight, 'dp', axis=1, tiled=True)]
    all_to_all x1 -> x0, blocking collectives: 48.7 us -> none  [body(): lax.all_to_all(outgoing, 'seq', split_axis=0, concat_axis=0, tiled=True)]
    ppermute x0 -> x9, starting transfers between devices: none -> 35.4 us  [the longest x3 23.8 us: ring_gather(): from_above = lax.ppermute(from_above, 'dp', down)]
    all_to_all x0 -> x2, starting transfers between devices: none -> 30.2 us  [the longest x1 17.5 us: step(): lax.all_to_all(send, 'seq', split_axis=0, concat_axis=0, tiled=True)]
    all_to_all x0 -> x2, waiting for transfers between devices: none -> 18.3 us  [the longest x1 18.3 us: step(): lax.all_to_all(late_send, 'seq', split_axis=0, concat_axis=0, tiled=True)]
    pallas_call x0 -> x6, Pallas kernels: none -> 15.1 us  [call(): pl.pallas_call(kernel, out_shape=out_shape, in_specs=[SMEM] * smem + [VME...]
    ppermute x0 -> x9, waiting for transfers between devices: none -> 14.7 us  [the longest x4 9.69 us: ring_gather(): from_below = lax.ppermute(from_below, 'dp', up)]
    dot_general x3 -> x0, matrix products: 6.15 us -> none  [the longest x1 3.3 us: body(): jnp.dot(context, lax.all_gather(out_weight, 'dp', axis=1, tiled=True), pr...]
  transfers between devices with their start and end apart: 1 -> 11, of which waited for: 1 -> 6; matrix products, arithmetic and copies ran while one was open for 6% -> 0% of each run, Pallas kernels for 0% -> 6%
where the time goes in v1:
time: 121 us; the launch traced here: 120 us
  starting transfers between devices  65.6 us (54%)
  waiting for transfers between devices  33.1 us (27%)
  Pallas kernels  15.1 us (12%)
  local copies, waits for them, and re-layouts  5.92 us (5%)
    ppermute x3, starting transfers between devices, ring_gather(): from_above = lax.ppermute(from_above, 'dp', down)  23.8 us
    all_to_all x1, waiting for transfers between devices, step(): lax.all_to_all(late_send, 'seq', split_axis=0, concat_axis=0, tiled=True)  18.3 us
    all_to_all x1, starting transfers between devices, step(): lax.all_to_all(send, 'seq', split_axis=0, concat_axis=0, tiled=True)  17.5 us
    pallas_call x6, Pallas kernels, call(): pl.pallas_call(kernel, out_shape=out_shape, in_specs=[SMEM] * smem + [VME...  15.1 us
    all_to_all x1, starting transfers between devices, step(): lax.all_to_all(late_send, 'seq', split_axis=0, concat_axis=0, tiled=True)  12.7 us
    ppermute x4, waiting for transfers between devices, ring_gather(): from_below = lax.ppermute(from_below, 'dp', up)  9.69 us
    ppermute x4, starting transfers between devices, ring_gather(): from_below = lax.ppermute(from_below, 'dp', up)  7.79 us
    unnamed x20, local copies, waits for them, and re-layouts  5.02 us
  transfers between devices with their start and end apart: 11, of which 6 were waited for; matrix products, arithmetic and copies ran while one was open for 0% of the time, Pallas kernels for 6%

profile of v1, /device:TPU:4, one launch (start us, length us, event | category | flops | bytes accessed | tf_op | source)
XLA Modules:
  0.0 120.0 jit_solution(2871323066316954586)
XLA Ops:
  0.0 0.7 broadcast_in_dim.7
  0.7 0.1 broadcast_in_dim.8.owner_row_ref.refs_10_
  0.8 0.1 broadcast_in_dim.10.owner_col_ref.refs_11_
  0.9 0.0 copy-start.2
  0.9 1.0 copy-done.2
  2.0 0.7 copy-done.7
  2.6 1.4 %copy-done.9 = bf16[192,3840]{1,0:T(8,128)(2,1)S(1)} copy-done((bf16[192,3840]{1,0:T(8,128)(2,1)S(1)}, bf16[192,3840]{1,0:T(8,128)(2,1)}, u32[]{:S(2)}) %copy-start.9) | copy-done | bytes 1474584
  4.0 5.1 %shard_map.76 = (bf16[192,1280]{1,0:T(8,128)(2,1)}, bf16[512,1280]{1,0:T(8,128)(2,1)}) custom-call(s32[1,4]{1,0:T(1,128)S(1)} %copy-done.7, s32[1,192]{1,0:T(1,128)S(1)} %broadcast_in_dim.8.owner_row_ref.refs_10_, s32[192,1]{1,0:T(8,128)S(1)} %broadcast_in_dim.10.owner_col_ref.refs_11_, bf16[192,3840]{1,0:T(8,128)(2,1)S(1)} %copy-done.9, ...), custom_call_target="tpu_custom_call" | custom-call | flops 2147483648 | bytes 1048576 | tf_op jit(solution)/shard_map/pallas_call | solution.py:32
  9.1 17.5 %all-to-all-start = ((bf16[64,8,1280]{2,1,0:T(8,128)(2,1)}), bf16[64,8,1280]{2,1,0:T(8,128)(2,1)S(1)}, u32[]{:S(2)}, u32[]{:S(2)}) async-start(bf16[64,8,1280]{2,1,0:T(8,128)(2,1)} %bitcast.1), calls=%async_computation | async-start | bytes 2621440 | tf_op jit(solution)/shard_map/all_to_all | solution.py:220
  26.6 0.0 copy-start.6
  26.6 0.0 copy-start.8
  26.7 2.1 %collective-permute-start.3 = (bf16[80,1280]{1,0:T(8,128)(2,1)S(1)}, bf16[80,1280]{1,0:T(8,128)(2,1)S(1)}, u32[]{:S(2)}, u32[]{:S(2)}) collective-permute-start(bf16[80,1280]{1,0:T(8,128)(2,1)S(1)} %bitcast.8), channel_id=1, source_target_pairs={{0,128},{64,192},{128,256},{192,320},{256,384},{320,448},{384,512}... | collective-permute-start | bytes 614408 | tf_op jit(solution)/shard_map/ppermute | solution.py:192
  28.7 13.5 %collective-permute-start = (bf16[80,1280]{1,0:T(8,128)(2,1)S(1)}, bf16[80,1280]{1,0:T(8,128)(2,1)S(1)}, u32[]{:S(2)}, u32[]{:S(2)}) collective-permute-start(bf16[80,1280]{1,0:T(8,128)(2,1)S(1)} %bitcast.9), channel_id=1, source_target_pairs={{0,896},{64,960},{128,0},{192,64},{256,128},{320,192},{384,256},{4... | collective-permute-start | bytes 614408 | tf_op jit(solution)/shard_map/ppermute | solution.py:195
  42.3 2.6 %collective-permute-done.3.refs_2_.refs_7_ = bf16[80,1280]{1,0:T(8,128)(2,1)S(1)} collective-permute-done((bf16[80,1280]{1,0:T(8,128)(2,1)S(1)}, bf16[80,1280]{1,0:T(8,128)(2,1)S(1)}, u32[]{:S(2)}, u32[]{:S(2)}) %collective-permute-start.3) | collective-permute-done | bytes 204832 | tf_op jit(solution)/shard_map/ppermute | solution.py:192
  44.8 1.9 %collective-permute-start.4 = (bf16[80,1280]{1,0:T(8,128)(2,1)S(1)}, bf16[80,1280]{1,0:T(8,128)(2,1)S(1)}, u32[]{:S(2)}, u32[]{:S(2)}) collective-permute-start(bf16[80,1280]{1,0:T(8,128)(2,1)S(1)} %collective-permute-done.3.refs_2_.refs_7_), channel_id=1, source_target_pairs={{0,128},{64,192},{128,256},{192,320},{256,384},{320,448},{384,512}... | collective-permute-start | bytes 614408 | tf_op jit(solution)/shard_map/ppermute | solution.py:192
  46.8 5.1 %collective-permute-start.1 = (bf16[80,1280]{1,0:T(8,128)(2,1)S(1)}, bf16[80,1280]{1,0:T(8,128)(2,1)S(1)}, u32[]{:S(2)}, u32[]{:S(2)}) collective-permute-start(bf16[80,1280]{1,0:T(8,128)(2,1)S(1)} %collective-permute-done.refs_1_), channel_id=1, source_target_pairs={{0,896},{64,960},{128,0},{192,64},{256,128},{320,192},{384,256},{4... | collective-permute-start | bytes 614408 | tf_op jit(solution)/shard_map/ppermute | solution.py:195
  51.9 1.8 %collective-permute-done.4.refs_4_.refs_6_ = bf16[80,1280]{1,0:T(8,128)(2,1)S(1)} collective-permute-done((bf16[80,1280]{1,0:T(8,128)(2,1)S(1)}, bf16[80,1280]{1,0:T(8,128)(2,1)S(1)}, u32[]{:S(2)}, u32[]{:S(2)}) %collective-permute-start.4) | collective-permute-done | bytes 204832 | tf_op jit(solution)/shard_map/ppermute | solution.py:192
  53.7 1.9 %collective-permute-start.5 = (bf16[80,1280]{1,0:T(8,128)(2,1)S(1)}, bf16[80,1280]{1,0:T(8,128)(2,1)S(1)}, u32[]{:S(2)}, u32[]{:S(2)}) collective-permute-start(bf16[80,1280]{1,0:T(8,128)(2,1)S(1)} %collective-permute-done.4.refs_4_.refs_6_), channel_id=1, source_target_pairs={{0,128},{64,192},{128,256},{192,320},{256,384},{320,448},{384,512}... | collective-permute-start | bytes 614408 | tf_op jit(solution)/shard_map/ppermute | solution.py:192
  55.6 0.1 shard_map.77
  55.7 1.9 %collective-permute-start.7 = (bf16[5,80,1280]{2,1,0:T(8,128)(2,1)S(1)}, bf16[5,80,1280]{2,1,0:T(8,128)(2,1)S(1)}, u32[]{:S(2)}, u32[]{:S(2)}) collective-permute-start(bf16[5,80,1280]{2,1,0:T(8,128)(2,1)S(1)} %shard_map.77), channel_id=1, source_target_pairs={{0,64},{64,0},{128,192},{192,128},{256,320},{320,256},{384,448},{4... | collective-permute-start | bytes 3072008 | tf_op jit(solution)/shard_map/ppermute | solution.py:199
  57.6 5.1 %collective-permute-start.2 = (bf16[80,1280]{1,0:T(8,128)(2,1)S(1)}, bf16[80,1280]{1,0:T(8,128)(2,1)S(1)}, u32[]{:S(2)}, u32[]{:S(2)}) collective-permute-start(bf16[80,1280]{1,0:T(8,128)(2,1)S(1)} %collective-permute-done.1.refs_3_.refs_2_), channel_id=1, source_target_pairs={{0,896},{64,960},{128,0},{192,64},{256,128},{320,192},{384,256},{4... | collective-permute-start | bytes 614408 | tf_op jit(solution)/shard_map/ppermute | solution.py:195
  62.8 1.9 %collective-permute-start.6 = (bf16[80,1280]{1,0:T(8,128)(2,1)S(1)}, bf16[80,1280]{1,0:T(8,128)(2,1)S(1)}, u32[]{:S(2)}, u32[]{:S(2)}) collective-permute-start(bf16[80,1280]{1,0:T(8,128)(2,1)S(1)} %collective-permute-done.5.refs_1_.refs_5_), channel_id=1, source_target_pairs={{0,128},{64,192},{128,256},{192,320},{256,384},{320,448},{384,512}... | collective-permute-start | bytes 614408 | tf_op jit(solution)/shard_map/ppermute | solution.py:192
  64.7 3.0 %collective-permute-done.2.refs_0_.refs_3_ = bf16[80,1280]{1,0:T(8,128)(2,1)S(1)} collective-permute-done((bf16[80,1280]{1,0:T(8,128)(2,1)S(1)}, bf16[80,1280]{1,0:T(8,128)(2,1)S(1)}, u32[]{:S(2)}, u32[]{:S(2)}) %collective-permute-start.2) | collective-permute-done | bytes 204832 | tf_op jit(solution)/shard_map/ppermute | solution.py:195
  67.7 5.3 %collective-permute-done.6.refs_2_.refs_4_ = bf16[80,1280]{1,0:T(8,128)(2,1)S(1)} collective-permute-done((bf16[80,1280]{1,0:T(8,128)(2,1)S(1)}, bf16[80,1280]{1,0:T(8,128)(2,1)S(1)}, u32[]{:S(2)}, u32[]{:S(2)}) %collective-permute-start.6) | collective-permute-done | bytes 204832 | tf_op jit(solution)/shard_map/ppermute | solution.py:192
  73.1 1.9 %collective-permute-start.8 = (bf16[3,80,1280]{2,1,0:T(8,128)(2,1)S(1)}, bf16[3,80,1280]{2,1,0:T(8,128)(2,1)S(1)}, u32[]{:S(2)}, u32[]{:S(2)}) collective-permute-start(bf16[3,80,1280]{2,1,0:T(8,128)(2,1)S(1)} %shard_map.78), channel_id=1, source_target_pairs={{0,64},{64,0},{128,192},{192,128},{256,320},{320,256},{384,448},{4... | collective-permute-start | bytes 1843208 | tf_op jit(solution)/shard_map/ppermute | solution.py:199
  75.1 2.0 %collective-permute-done.8.refs_9_ = bf16[3,80,1280]{2,1,0:T(8,128)(2,1)S(1)} collective-permute-done((bf16[3,80,1280]{2,1,0:T(8,128)(2,1)S(1)}, bf16[3,80,1280]{2,1,0:T(8,128)(2,1)S(1)}, u32[]{:S(2)}, u32[]{:S(2)}) %collective-permute-start.8) | collective-permute-done | bytes 614432 | tf_op jit(solution)/shard_map/ppermute | solution.py:199
  77.1 5.2 %shard_map.79 = (bf16[1280,1280]{1,0:T(8,128)(2,1)}, bf16[512,640]{1,0:T(8,128)(2,1)}) custom-call(s32[1,4]{1,0:T(1,128)S(1)} %copy-done.8, bf16[80,1280]{1,0:T(8,128)(2,1)S(1)} %bitcast.11, bf16[80,1280]{1,0:T(8,128)(2,1)S(1)} %collective-permute-done.refs_1_, bf16[80,1280]{1,0:T(8,128)(2,1)S(1)} %collective-permute-done.1.refs_3_.refs_2_, ...), custom_call_target="tpu_custom_call" | custom-call | flops 629145600 | bytes 1048576 | tf_op jit(solution)/shard_map/pallas_call | solution.py:32
  82.4 12.7 %all-to-all-start.1 = ((bf16[64,8,640]{2,1,0:T(8,128)(2,1)}), bf16[64,8,640]{2,1,0:T(8,128)(2,1)S(1)}, u32[]{:S(2)}, u32[]{:S(2)}) async-start(bf16[64,8,640]{2,1,0:T(8,128)(2,1)} %bitcast.4), calls=%async_computation.1 | async-start | bytes 1310720 | tf_op jit(solution)/shard_map/all_to_all | solution.py:230
  95.1 1.9 %copy-done = bf16[1280,1280]{1,0:T(8,128)(2,1)S(1)} copy-done((bf16[1280,1280]{1,0:T(8,128)(2,1)S(1)}, bf16[1280,1280]{1,0:T(8,128)(2,1)}, u32[]{:S(2)}) %copy-start) | copy-done | bytes 3276824
  97.0 2.2 %shard_map.80.normed_ref = bf16[256,1280]{1,0:T(8,128)(2,1)S(1)} custom-call(bf16[512,1280]{1,0:T(8,128)(2,1)S(1)} %bitcast.6, bf16[1280,1280]{1,0:T(8,128)(2,1)S(1)} %copy-done, f32[1280]{0:T(1024)S(1)} %copy-done.5, f32[1280]{0:T(1024)S(1)} %copy-done.6), custom_call_target="tpu_custom_call" | custom-call | flops 838860800 | bytes 1048576 | tf_op jit(solution)/shard_map/pallas_call | solution.py:32
  99.2 18.3 %all-to-all-done.1 = bf16[64,8,640]{2,1,0:T(8,128)(2,1)S(1)} async-done(((bf16[64,8,640]{2,1,0:T(8,128)(2,1)}), bf16[64,8,640]{2,1,0:T(8,128)(2,1)S(1)}, u32[]{:S(2)}, u32[]{:S(2)}) %all-to-all-start.1) | async-done | bytes 655392 | tf_op jit(solution)/shard_map/all_to_all | solution.py:230
  117.5 2.5 %shard_map.81 = bf16[128,5120]{1,0:T(8,128)(2,1)} custom-call(bf16[256,1280]{1,0:T(8,128)(2,1)S(1)} %shard_map.80.normed_ref, bf16[512,640]{1,0:T(8,128)(2,1)S(1)} %bitcast.7), custom_call_target="tpu_custom_call" | custom-call | flops 536870912 | bytes 1048576 | tf_op jit(solution)/shard_map/pallas_call | solution.py:32
  (19 shorter events, 0.1 us)
Async XLA Ops:
  0.9 1.0 copy-start.2
  2.0 0.7 copy-start.7
  2.6 1.4 %copy-start.9 = (bf16[192,3840]{1,0:T(8,128)(2,1)S(1)}, bf16[192,3840]{1,0:T(8,128)(2,1)}, u32[]{:S(2)}) copy-start(bf16[192,3840]{1,0:T(8,128)(2,1)} %packed_ref.1) | copy-start | bytes 4423684
  9.1 17.5 %copy-start.1 = (bf16[1280,80]{0,1:T(8,128)(2,1)S(1)}, bf16[1280,80]{0,1:T(8,128)(2,1)}, u32[]{:S(2)}) copy-start(bf16[1280,80]{0,1:T(8,128)(2,1)} %param.11) | copy-start | bytes 614404
  9.1 73.2 %all-to-all-start = ((bf16[64,8,1280]{2,1,0:T(8,128)(2,1)}), bf16[64,8,1280]{2,1,0:T(8,128)(2,1)S(1)}, u32[]{:S(2)}, u32[]{:S(2)}) async-start(bf16[64,8,1280]{2,1,0:T(8,128)(2,1)} %bitcast.1), calls=%async_computation | async-start | bytes 2621440 | tf_op jit(solution)/shard_map/all_to_all | solution.py:220
  26.6 50.5 %copy-start.3 = (bf16[192,1280]{1,0:T(8,128)(2,1)S(1)}, bf16[192,1280]{1,0:T(8,128)(2,1)}, u32[]{:S(2)}) copy-start(bf16[192,1280]{1,0:T(8,128)(2,1)} %refs_13_.1) | copy-start | bytes 1474564
  26.6 50.4 %copy-start.4 = (bf16[192,1280]{1,0:T(8,128)(2,1)S(1)}, bf16[192,1280]{1,0:T(8,128)(2,1)}, u32[]{:S(2)}) copy-start(bf16[192,1280]{1,0:T(8,128)(2,1)} %get-tuple-element.10.refs_12_) | copy-start | bytes 1474564
  26.6 50.4 %copy-start.5 = (f32[1280]{0:T(1024)S(1)}, f32[1280]{0:T(1024)}, u32[]{:S(2)}) copy-start(f32[1280]{0:T(1024)} %gain_ref.1) | copy-start | bytes 15364
  26.6 50.4 %copy-start.6 = (f32[1280]{0:T(1024)S(1)}, f32[1280]{0:T(1024)}, u32[]{:S(2)}) copy-start(f32[1280]{0:T(1024)} %bias_ref.1) | copy-start | bytes 15364
  26.6 50.4 %copy-start.8 = (s32[1,4]{1,0:T(1,128)S(1)}, s32[1,4]{1,0:T(1,128)}, u32[]{:S(2)}) copy-start(s32[1,4]{1,0:T(1,128)} %counts_ref.3) | copy-start | bytes 52
  26.7 18.2 %collective-permute-start.3 = (bf16[80,1280]{1,0:T(8,128)(2,1)S(1)}, bf16[80,1280]{1,0:T(8,128)(2,1)S(1)}, u32[]{:S(2)}, u32[]{:S(2)}) collective-permute-start(bf16[80,1280]{1,0:T(8,128)(2,1)S(1)} %bitcast.8), channel_id=1, source_target_pairs={{0,128},{64,192},{128,256},{192,320},{256,384},{320,448},{384,512}... | collective-permute-start | bytes 614408 | tf_op jit(solution)/shard_map/ppermute | solution.py:192
  28.7 18.0 %collective-permute-start = (bf16[80,1280]{1,0:T(8,128)(2,1)S(1)}, bf16[80,1280]{1,0:T(8,128)(2,1)S(1)}, u32[]{:S(2)}, u32[]{:S(2)}) collective-permute-start(bf16[80,1280]{1,0:T(8,128)(2,1)S(1)} %bitcast.9), channel_id=1, source_target_pairs={{0,896},{64,960},{128,0},{192,64},{256,128},{320,192},{384,256},{4... | collective-permute-start | bytes 614408 | tf_op jit(solution)/shard_map/ppermute | solution.py:195
  44.8 8.9 %collective-permute-start.4 = (bf16[80,1280]{1,0:T(8,128)(2,1)S(1)}, bf16[80,1280]{1,0:T(8,128)(2,1)S(1)}, u32[]{:S(2)}, u32[]{:S(2)}) collective-permute-start(bf16[80,1280]{1,0:T(8,128)(2,1)S(1)} %collective-permute-done.3.refs_2_.refs_7_), channel_id=1, source_target_pairs={{0,128},{64,192},{128,256},{192,320},{256,384},{320,448},{384,512}... | collective-permute-start | bytes 614408 | tf_op jit(solution)/shard_map/ppermute | solution.py:192
  46.8 8.8 %collective-permute-start.1 = (bf16[80,1280]{1,0:T(8,128)(2,1)S(1)}, bf16[80,1280]{1,0:T(8,128)(2,1)S(1)}, u32[]{:S(2)}, u32[]{:S(2)}) collective-permute-start(bf16[80,1280]{1,0:T(8,128)(2,1)S(1)} %collective-permute-done.refs_1_), channel_id=1, source_target_pairs={{0,896},{64,960},{128,0},{192,64},{256,128},{320,192},{384,256},{4... | collective-permute-start | bytes 614408 | tf_op jit(solution)/shard_map/ppermute | solution.py:195
  53.7 9.1 %collective-permute-start.5 = (bf16[80,1280]{1,0:T(8,128)(2,1)S(1)}, bf16[80,1280]{1,0:T(8,128)(2,1)S(1)}, u32[]{:S(2)}, u32[]{:S(2)}) collective-permute-start(bf16[80,1280]{1,0:T(8,128)(2,1)S(1)} %collective-permute-done.4.refs_4_.refs_6_), channel_id=1, source_target_pairs={{0,128},{64,192},{128,256},{192,320},{256,384},{320,448},{384,512}... | collective-permute-start | bytes 614408 | tf_op jit(solution)/shard_map/ppermute | solution.py:192
  55.7 21.4 %collective-permute-start.7 = (bf16[5,80,1280]{2,1,0:T(8,128)(2,1)S(1)}, bf16[5,80,1280]{2,1,0:T(8,128)(2,1)S(1)}, u32[]{:S(2)}, u32[]{:S(2)}) collective-permute-start(bf16[5,80,1280]{2,1,0:T(8,128)(2,1)S(1)} %shard_map.77), channel_id=1, source_target_pairs={{0,64},{64,0},{128,192},{192,128},{256,320},{320,256},{384,448},{4... | collective-permute-start | bytes 3072008 | tf_op jit(solution)/shard_map/ppermute | solution.py:199
  57.6 10.1 %collective-permute-start.2 = (bf16[80,1280]{1,0:T(8,128)(2,1)S(1)}, bf16[80,1280]{1,0:T(8,128)(2,1)S(1)}, u32[]{:S(2)}, u32[]{:S(2)}) collective-permute-start(bf16[80,1280]{1,0:T(8,128)(2,1)S(1)} %collective-permute-done.1.refs_3_.refs_2_), channel_id=1, source_target_pairs={{0,896},{64,960},{128,0},{192,64},{256,128},{320,192},{384,256},{4... | collective-permute-start | bytes 614408 | tf_op jit(solution)/shard_map/ppermute | solution.py:195
  62.8 10.3 %collective-permute-start.6 = (bf16[80,1280]{1,0:T(8,128)(2,1)S(1)}, bf16[80,1280]{1,0:T(8,128)(2,1)S(1)}, u32[]{:S(2)}, u32[]{:S(2)}) collective-permute-start(bf16[80,1280]{1,0:T(8,128)(2,1)S(1)} %collective-permute-done.5.refs_1_.refs_5_), channel_id=1, source_target_pairs={{0,128},{64,192},{128,256},{192,320},{256,384},{320,448},{384,512}... | collective-permute-start | bytes 614408 | tf_op jit(solution)/shard_map/ppermute | solution.py:192
  73.1 3.9 %collective-permute-start.8 = (bf16[3,80,1280]{2,1,0:T(8,128)(2,1)S(1)}, bf16[3,80,1280]{2,1,0:T(8,128)(2,1)S(1)}, u32[]{:S(2)}, u32[]{:S(2)}) collective-permute-start(bf16[3,80,1280]{2,1,0:T(8,128)(2,1)S(1)} %shard_map.78), channel_id=1, source_target_pairs={{0,64},{64,0},{128,192},{192,128},{256,320},{320,256},{384,448},{4... | collective-permute-start | bytes 1843208 | tf_op jit(solution)/shard_map/ppermute | solution.py:199
  82.4 35.2 %all-to-all-start.1 = ((bf16[64,8,640]{2,1,0:T(8,128)(2,1)}), bf16[64,8,640]{2,1,0:T(8,128)(2,1)S(1)}, u32[]{:S(2)}, u32[]{:S(2)}) async-start(bf16[64,8,640]{2,1,0:T(8,128)(2,1)} %bitcast.4), calls=%async_computation.1 | async-start | bytes 1310720 | tf_op jit(solution)/shard_map/all_to_all | solution.py:230
  95.1 1.9 %copy-start = (bf16[1280,1280]{1,0:T(8,128)(2,1)S(1)}, bf16[1280,1280]{1,0:T(8,128)(2,1)}, u32[]{:S(2)}) copy-start(bf16[1280,1280]{1,0:T(8,128)(2,1)} %get-tuple-element.11.weight_ref) | copy-start | bytes 9830404

commit v2 on v1

v2 whole, which is shorter than its diff:
```python
import functools

import jax
import jax.numpy as jnp
from jax import lax
from jax.experimental import pallas as pl
from jax.experimental.pallas import tpu as pltpu
from jax.sharding import PartitionSpec as P


HEADS = 16
IMGS = 4
DEAD = -1000
VMEM = pl.BlockSpec(memory_space=pltpu.VMEM)
SMEM = pl.BlockSpec(memory_space=pltpu.SMEM)
HBM = pl.BlockSpec(memory_space=pltpu.HBM)
F32 = jnp.float32
BF16 = jnp.bfloat16


def iota(shape, dim):
    return lax.broadcasted_iota(jnp.int32, shape, dim)


def pick(hits, values):
    return lax.dot_general(
        jnp.where(hits, 1.0, 0.0).astype(BF16), values, (((1,), (0,)), ((), ())), preferred_element_type=F32
    )


def call(kernel, out_shape, operands, flops, scratch=(), smem=0, limit=8, out_specs=VMEM, in_specs=None):
    return pl.pallas_call(
        kernel,
        out_shape=out_shape,
        in_specs=in_specs or [SMEM] * smem + [VMEM] * (len(operands) - smem),
        out_specs=out_specs,
        scratch_shapes=list(scratch),
        compiler_params=pltpu.CompilerParams(vmem_limit_bytes=limit * 1024 * 1024),
        cost_estimate=pl.CostEstimate(flops=flops, bytes_accessed=1 << 20, transcendentals=0),
    )(*operands)


def image_ends(counts_ref):
    ends, end = [], 0
    for image in range(IMGS):
        end = end + counts_ref[0, image]
        ends.append(end)
    return ends


def row_slots(ends, owner_ref, rows):
    groups = owner_ref.shape[1]
    lane, sub = iota((1, rows), 1), iota((rows, 1), 0)
    owners = jnp.broadcast_to(owner_ref[...], (8, groups)).astype(F32).astype(BF16)
    spread = jnp.where((iota((1, rows), 1) >> 2) == iota((groups, 1), 0), 1.0, 0.0).astype(BF16)
    owner_row = jnp.dot(owners, spread, preferred_element_type=F32)[0:1, :]
    owner_col = jnp.sum(jnp.where(sub == lane, owner_row, 0.0), axis=1, keepdims=True)
    first = lane - (lane & 3)
    earlier = (owner_col == owner_row) & (sub < first) & ((sub & 3) == 0) & (sub < ends[-1])
    slot = jnp.sum(jnp.where(earlier, 1.0, 0.0), axis=0, keepdims=True)
    return owner_row.astype(jnp.int32), slot, first < ends[-1], lane & 3


def front_kernel(
    counts_in, owner_in, packed_in, patch_in, context_out, send_ref,
    counts_ref, owner_ref, packed_ref, patch_ref, context_ref, done
):
    rows, width = patch_ref.shape
    head_size = width // HEADS
    pairs = ((counts_in, counts_ref), (packed_in, packed_ref), (owner_in, owner_ref), (patch_in, patch_ref))
    fetches = [pltpu.make_async_copy(src, dst, done.at[i]) for i, (src, dst) in enumerate(pairs)]
    for fetch in fetches:
        fetch.start()
    context_ref[...] = jnp.zeros_like(context_ref)
    fetches[0].wait()
    fetches[1].wait()
    ends = image_ends(counts_ref)
    lane, sub = iota((1, rows), 1), iota((rows, 1), 0)
    segment_row = sum((lane >= end).astype(jnp.int32) for end in ends)
    segment_col = sum((sub >= end).astype(jnp.int32) for end in ends)
    same_image = segment_col == segment_row
    for head in range(HEADS):
        low = head * head_size
        start = min(low // 128 * 128, width - 256)
        column = iota((1, 256), 1) + start
        mine = (column >= low) & (column < low + head_size)
        queries = packed_ref[:, start : start + 256]
        queries = jnp.where(mine, queries, jnp.zeros_like(queries))
        keys = packed_ref[:, width + start : width + start + 256]
        scores = lax.dot_general(
            queries, keys, (((1,), (1,)), ((), ())), preferred_element_type=F32
        ) * head_size ** (-0.5)
        scores = jnp.where(same_image, scores, -1e30)
        expo = jnp.exp(scores - jnp.max(scores, axis=1, keepdims=True))
        weights = (expo / jnp.sum(expo, axis=1, keepdims=True)).astype(BF16)
        values = packed_ref[:, 2 * width + start : 2 * width + start + 256]
        mixed = jnp.dot(weights, values, preferred_element_type=F32).astype(BF16)
        context_ref[:, start : start + 256] = jnp.where(mine, mixed, context_ref[:, start : start + 256])
    leave = pltpu.make_async_copy(context_ref, context_out, done.at[4])
    leave.start()
    fetches[2].wait()
    fetches[3].wait()
    owner_row, slot, live, part = row_slots(ends, owner_ref, rows)
    key = jnp.where(live & (slot == 0.0), owner_row * 8 + part, DEAD)
    line = iota((send_ref.shape[0], 1), 0)
    hits = key == line
    held = jnp.sum(jnp.where(hits, 1.0, 0.0), axis=1, keepdims=True)
    marker = jnp.where((held == 0.0) & ((line & 7) < 4), 64.0, 0.0)
    sent = pick(hits, patch_ref[...]) + pick(key == line - 4, context_ref[...]) + marker
    send_ref[...] = sent.astype(BF16)
    leave.wait()


def norm(hidden, gain, bias):
    gain, bias = gain[None, :], bias[None, :]
    inverse = 1.0 / hidden.shape[1]
    centered = hidden - jnp.sum(hidden, axis=1, keepdims=True) * inverse
    row_var = jnp.sum(centered * centered, axis=1, keepdims=True) * inverse
    return centered * lax.rsqrt(row_var + 1e-06) * gain + bias


def project(context, weight):
    return lax.dot_general(context, weight, (((1,), (1,)), ((), ())), preferred_element_type=F32)


def late_kernel(nz, splits, counts_ref, *refs):
    blocks, refs = refs[:nz], refs[nz:]
    halves, refs = refs[: len(splits)], refs[len(splits) :]
    owner_ref, context_ref, patch_ref, gain_ref, bias_ref = refs[:5]
    weight_out, send_ref, weight_ref, done = refs[5:]
    block_width = blocks[0].shape[0]
    me = lax.axis_index("dp")
    z, c = lax.shift_right_logical(me, 1), lax.bitwise_and(me, 1)
    pieces = [(j, c, blocks[j]) for j in range(nz)]
    for part, ref in zip(splits, halves):
        pieces += [(j, 1 - c, ref.at[i]) for i, j in enumerate(part)]
    leaves, places = [], []
    for i, (j, core, ref) in enumerate(pieces):
        owner = lax.rem(z + j * (1 - 2 * core) + nz, nz) * 2 + core
        places.append(pl.ds(pl.multiple_of(owner * block_width, 16), block_width))
        leaves.append(pltpu.make_async_copy(ref, weight_out.at[places[i], :], done.at[i]))
        leaves[i].start()
    for place, (_, _, ref) in zip(places, pieces):
        weight_ref[place, :] = ref[...]
    hidden = patch_ref[...].astype(F32) + project(context_ref[...], weight_ref[...])
    normed = norm(hidden, gain_ref[...], bias_ref[...]).astype(BF16)
    owner_row, slot, live, part = row_slots(image_ends(counts_ref), owner_ref, patch_ref.shape[0])
    key = jnp.where(live & (slot == 1.0), owner_row * 8 + 2 * part, DEAD)
    line = iota((send_ref.shape[0], 1), 0)
    half = send_ref.shape[1]
    sent = pick(key == line, normed[:, :half]) + pick(key == line - 1, normed[:, half:])
    send_ref[...] = sent.astype(BF16)
    for leave in leaves:
        leave.wait()


def early_kernel(received_ref, weight_ref, gain_ref, bias_ref, out_ref):
    lines, width = received_ref.shape
    owners = lines // 8
    row = iota((4 * owners, 1), 0)
    place = (row & (owners - 1)) * 8 + (row >> (owners.bit_length() - 1))
    column = iota((1, lines), 1)
    patches = pick(column == place, received_ref[...])
    context = pick(column == place + 4, received_ref[...]).astype(BF16)
    normed = norm(patches + project(context, weight_ref[...]), gain_ref[...], bias_ref[...])
    normed = jnp.where(patches[:, :1] > 32.0, 0.0, normed).astype(BF16)
    even = iota((2 * owners, 1), 0) == 2 * iota((1, owners), 1)
    for part in range(4):
        first = pick(even, normed[part * owners : (part + 1) * owners, :])
        out_ref[:, part * width : (part + 1) * width] = first.astype(BF16)


def join_kernel(first_ref, received_ref, out_ref, joined_ref, done):
    lines, half = received_ref.shape
    slots = lines // 4
    row = iota((8 * slots, 1), 0)
    slot, chunk = row & (slots - 1), row >> (slots.bit_length() - 1)
    hits = (iota((1, lines), 1) == 4 * (slot - 1) + chunk) & ((slot & 1) == 1)
    second = pick(hits, received_ref[...]).astype(BF16)
    leaves = []
    for i in range(8):
        columns = slice(i * half, (i + 1) * half)
        joined_ref[:, columns] = first_ref[:, columns] + second[i * slots : (i + 1) * slots]
        leave = pltpu.make_async_copy(joined_ref.at[:, columns], out_ref.at[:, columns], done.at[i])
        leave.start()
        leaves.append(leave)
    for leave in leaves:
        leave.wait()


def pack_kernel(*refs):
    for i, ref in enumerate(refs[:-1]):
        refs[-1][i] = ref[...]


def pack(blocks):
    shape = jax.ShapeDtypeStruct((len(blocks), *blocks[0].shape), blocks[0].dtype)
    return call(pack_kernel, shape, blocks, 1 << 20, limit=1)


def ring_gather(shard):
    n_dp = lax.axis_size("dp")
    nz = n_dp // 2
    up = [(2 * z + c, 2 * ((z + 1 - 2 * c) % nz) + c) for z in range(nz) for c in range(2)]
    down = [(there, here) for here, there in up]
    swap = [(d, d ^ 1) for d in range(n_dp)]
    blocks = [None] * nz
    blocks[0] = shard
    from_below, from_above = shard, shard
    for step in range(1, nz // 2 + 1):
        from_below = lax.ppermute(from_below, "dp", up)
        blocks[(-step) % nz] = from_below
        if step < nz - step:
            from_above = lax.ppermute(from_above, "dp", down)
            blocks[step] = from_above
    order = sorted(range(nz), key=lambda j: min(j, nz - j))
    splits = [s for s in (order[: nz // 2 + 1], order[nz // 2 + 1 :]) if s]
    halves = [lax.ppermute(pack([blocks[j] for j in part]), "dp", swap) for part in splits]
    return blocks, splits, halves


def step(patches, query_key_value, counts, owner_index, out_weight, ln_gain, ln_bias):
    rows, width = patches.shape
    owners = lax.axis_size("seq")
    nz = lax.axis_size("dp") // 2
    owner_lanes = owner_index.reshape(1, rows // 4)
    lines = 8 * owners

    blocks, splits, halves = ring_gather(out_weight.T)
    context, send = call(
        front_kernel,
        (pltpu.HBM((rows, width), BF16), jax.ShapeDtypeStruct((lines, width), BF16)),
        [pltpu.with_memory_space_constraint(x, pltpu.HBM) for x in (counts, owner_lanes, query_key_value, patches)],
        1 << 31,
        scratch=[
            pltpu.SMEM(counts.shape, jnp.int32),
            pltpu.VMEM(owner_lanes.shape, jnp.int32),
            pltpu.VMEM((rows, 3 * width), BF16),
            pltpu.VMEM((rows, width), BF16),
            pltpu.VMEM((rows, width), BF16),
            pltpu.SemaphoreType.DMA((5,)),
        ],
        out_specs=(HBM, VMEM),
        in_specs=[HBM] * 4,
        limit=16,
    )
    received = lax.all_to_all(send, "seq", split_axis=0, concat_axis=0, tiled=True)
    weight, late_send = call(
        functools.partial(late_kernel, nz, splits),
        (pltpu.HBM((width, width), BF16), jax.ShapeDtypeStruct((lines, width // 2), BF16)),
        [counts, *blocks, *halves, owner_lanes, context, patches, ln_gain, ln_bias],
        2 * rows * width * width,
        scratch=[pltpu.VMEM((width, width), BF16), pltpu.SemaphoreType.DMA((2 * nz,))],
        smem=1,
        out_specs=(HBM, VMEM),
    )
    late_received = lax.all_to_all(late_send, "seq", split_axis=0, concat_axis=0, tiled=True)
    shape = jax.ShapeDtypeStruct((2 * owners, 4 * width), BF16)
    first = call(early_kernel, shape, [received, weight, ln_gain, ln_bias], 1 << 31)
    return call(
        join_kernel,
        pltpu.HBM(shape.shape, BF16),
        [first, late_received],
        1 << 29,
        scratch=[pltpu.VMEM(shape.shape, BF16), pltpu.SemaphoreType.DMA((8,))],
        out_specs=HBM,
    )


def solution(mesh):
    placed = (
        P(("dp", "seq"), None),
        P(("dp", "seq"), None),
        P(("dp", "seq"), None),
        P(("dp", "seq"), None),
        P(None, "dp"),
        P(),
        P(),
    )
    return jax.shard_map(step, mesh=mesh, in_specs=placed, out_specs=P(("dp", "seq"), None), check_vma=False)
```

time: 121 us -> 116 us (0.959)
  local copies, waits for them, and re-layouts: 5.92 us -> 1.96 us
  waiting for transfers between devices: 33.1 us -> 31 us
    unnamed x20 -> x16, local copies, waits for them, and re-layouts: 5.02 us -> 1.96 us
  transfers between devices with their start and end apart: 11 -> 11, of which waited for: 6 -> 6; matrix products, arithmetic and copies ran while one was open for 0% -> 0% of each run, Pallas kernels for 6% -> 7%
where the time goes in v2:
time: 116 us
  starting transfers between devices  66.4 us (57%)
  waiting for transfers between devices  31 us (27%)
  Pallas kernels  16.1 us (14%)
  local copies, waits for them, and re-layouts  1.96 us (2%)
    ppermute x3, starting transfers between devices, ring_gather(): from_above = lax.ppermute(from_above, 'dp', down)  24.5 us
    all_to_all x1, waiting for transfers between devices, step(): lax.all_to_all(late_send, 'seq', split_axis=0, concat_axis=0, tiled=True)  17.8 us
    all_to_all x1, starting transfers between devices, step(): lax.all_to_all(send, 'seq', split_axis=0, concat_axis=0, tiled=True)  17.5 us
    pallas_call x6, Pallas kernels, call(): pl.pallas_call(kernel, out_shape=out_shape, in_specs=in_specs or [SMEM] *...  16.1 us
    all_to_all x1, starting transfers between devices, step(): lax.all_to_all(late_send, 'seq', split_axis=0, concat_axis=0, tiled=True)  12.7 us
    ppermute x4, waiting for transfers between devices, ring_gather(): from_below = lax.ppermute(from_below, 'dp', up)  9.09 us
    ppermute x4, starting transfers between devices, ring_gather(): from_below = lax.ppermute(from_below, 'dp', up)  7.79 us
    ppermute x2, starting transfers between devices, ring_gather(): lax.ppermute(pack([blocks[j] for j in part]), 'dp', swap)  3.84 us
  transfers between devices with their start and end apart: 11, of which 6 were waited for; matrix products, arithmetic and copies ran while one was open for 0% of the time, Pallas kernels for 7%

profile of v2, /device:TPU:4, one launch (start us, length us, event | category | flops | bytes accessed | tf_op | source)
XLA Modules:
  0.0 115.6 jit_solution(15143529690987400073)
XLA Ops:
  0.0 5.9 %shard_map.73 = (bf16[192,1280]{1,0:T(8,128)(2,1)}, bf16[512,1280]{1,0:T(8,128)(2,1)}) custom-call(s32[1,4]{1,0:T(1,128)} %counts_ref.1, s32[1,48]{1,0:T(1,128)} %bitcast.12, bf16[192,3840]{1,0:T(8,128)(2,1)} %packed_in.1, bf16[192,1280]{1,0:T(8,128)(2,1)} %refs_12_.1), custom_call_target="tpu_custom_call" | custom-call | flops 2147483648 | bytes 1048576 | tf_op jit(solution)/shard_map/pallas_call | solution.py:32
  5.9 0.0 copy-start
  5.9 17.5 %all-to-all-start = ((bf16[64,8,1280]{2,1,0:T(8,128)(2,1)}), bf16[64,8,1280]{2,1,0:T(8,128)(2,1)S(1)}, u32[]{:S(2)}, u32[]{:S(2)}) async-start(bf16[64,8,1280]{2,1,0:T(8,128)(2,1)} %bitcast.1), calls=%async_computation | async-start | bytes 2621440 | tf_op jit(solution)/shard_map/all_to_all | solution.py:247
  23.4 0.0 copy-start.1
  23.4 0.0 copy-start.3
  23.4 0.0 copy-start.4
  23.4 0.0 copy-start.5
  23.4 0.0 copy-start.6
  23.5 2.1 %collective-permute-start.3 = (bf16[80,1280]{1,0:T(8,128)(2,1)S(1)}, bf16[80,1280]{1,0:T(8,128)(2,1)S(1)}, u32[]{:S(2)}, u32[]{:S(2)}) collective-permute-start(bf16[80,1280]{1,0:T(8,128)(2,1)S(1)} %bitcast.8), channel_id=1, source_target_pairs={{0,128},{64,960},{128,256},{192,64},{256,384},{320,192},{384,512},... | collective-permute-start | bytes 614408 | tf_op jit(solution)/shard_map/ppermute | solution.py:211
  25.5 13.5 %collective-permute-start = (bf16[80,1280]{1,0:T(8,128)(2,1)S(1)}, bf16[80,1280]{1,0:T(8,128)(2,1)S(1)}, u32[]{:S(2)}, u32[]{:S(2)}) collective-permute-start(bf16[80,1280]{1,0:T(8,128)(2,1)S(1)} %bitcast.9), channel_id=1, source_target_pairs={{128,0},{960,64},{256,128},{64,192},{384,256},{192,320},{512,384},... | collective-permute-start | bytes 614408 | tf_op jit(solution)/shard_map/ppermute | solution.py:214
  39.0 1.8 %collective-permute-done.3.refs_2_.refs_7_ = bf16[80,1280]{1,0:T(8,128)(2,1)S(1)} collective-permute-done((bf16[80,1280]{1,0:T(8,128)(2,1)S(1)}, bf16[80,1280]{1,0:T(8,128)(2,1)S(1)}, u32[]{:S(2)}, u32[]{:S(2)}) %collective-permute-start.3) | collective-permute-done | bytes 204832 | tf_op jit(solution)/shard_map/ppermute | solution.py:211
  40.8 1.9 %collective-permute-start.4 = (bf16[80,1280]{1,0:T(8,128)(2,1)S(1)}, bf16[80,1280]{1,0:T(8,128)(2,1)S(1)}, u32[]{:S(2)}, u32[]{:S(2)}) collective-permute-start(bf16[80,1280]{1,0:T(8,128)(2,1)S(1)} %collective-permute-done.3.refs_2_.refs_7_), channel_id=1, source_target_pairs={{0,128},{64,960},{128,256},{192,64},{256,384},{320,192},{384,512},... | collective-permute-start | bytes 614408 | tf_op jit(solution)/shard_map/ppermute | solution.py:211
  42.8 5.9 %collective-permute-start.1 = (bf16[80,1280]{1,0:T(8,128)(2,1)S(1)}, bf16[80,1280]{1,0:T(8,128)(2,1)S(1)}, u32[]{:S(2)}, u32[]{:S(2)}) collective-permute-start(bf16[80,1280]{1,0:T(8,128)(2,1)S(1)} %collective-permute-done.refs_1_), channel_id=1, source_target_pairs={{128,0},{960,64},{256,128},{64,192},{384,256},{192,320},{512,384},... | collective-permute-start | bytes 614408 | tf_op jit(solution)/shard_map/ppermute | solution.py:214
  48.7 2.4 %collective-permute-done.4.refs_4_.refs_6_ = bf16[80,1280]{1,0:T(8,128)(2,1)S(1)} collective-permute-done((bf16[80,1280]{1,0:T(8,128)(2,1)S(1)}, bf16[80,1280]{1,0:T(8,128)(2,1)S(1)}, u32[]{:S(2)}, u32[]{:S(2)}) %collective-permute-start.4) | collective-permute-done | bytes 204832 | tf_op jit(solution)/shard_map/ppermute | solution.py:211
  51.0 1.9 %collective-permute-start.5 = (bf16[80,1280]{1,0:T(8,128)(2,1)S(1)}, bf16[80,1280]{1,0:T(8,128)(2,1)S(1)}, u32[]{:S(2)}, u32[]{:S(2)}) collective-permute-start(bf16[80,1280]{1,0:T(8,128)(2,1)S(1)} %collective-permute-done.4.refs_4_.refs_6_), channel_id=1, source_target_pairs={{0,128},{64,960},{128,256},{192,64},{256,384},{320,192},{384,512},... | collective-permute-start | bytes 614408 | tf_op jit(solution)/shard_map/ppermute | solution.py:211
  53.0 0.0 collective-permute-done.1.refs_3_.refs_2_
  53.0 0.1 shard_map.74
  53.1 1.9 %collective-permute-start.7 = (bf16[5,80,1280]{2,1,0:T(8,128)(2,1)S(1)}, bf16[5,80,1280]{2,1,0:T(8,128)(2,1)S(1)}, u32[]{:S(2)}, u32[]{:S(2)}) collective-permute-start(bf16[5,80,1280]{2,1,0:T(8,128)(2,1)S(1)} %shard_map.74), channel_id=1, source_target_pairs={{0,64},{64,0},{128,192},{192,128},{256,320},{320,256},{384,448},{4... | collective-permute-start | bytes 3072008 | tf_op jit(solution)/shard_map/ppermute | solution.py:218
  55.0 5.1 %collective-permute-start.2 = (bf16[80,1280]{1,0:T(8,128)(2,1)S(1)}, bf16[80,1280]{1,0:T(8,128)(2,1)S(1)}, u32[]{:S(2)}, u32[]{:S(2)}) collective-permute-start(bf16[80,1280]{1,0:T(8,128)(2,1)S(1)} %collective-permute-done.1.refs_3_.refs_2_), channel_id=1, source_target_pairs={{128,0},{960,64},{256,128},{64,192},{384,256},{192,320},{512,384},... | collective-permute-start | bytes 614408 | tf_op jit(solution)/shard_map/ppermute | solution.py:214
  60.1 0.0 collective-permute-done.5.refs_1_.refs_5_
  60.1 1.9 %collective-permute-start.6 = (bf16[80,1280]{1,0:T(8,128)(2,1)S(1)}, bf16[80,1280]{1,0:T(8,128)(2,1)S(1)}, u32[]{:S(2)}, u32[]{:S(2)}) collective-permute-start(bf16[80,1280]{1,0:T(8,128)(2,1)S(1)} %collective-permute-done.5.refs_1_.refs_5_), channel_id=1, source_target_pairs={{0,128},{64,960},{128,256},{192,64},{256,384},{320,192},{384,512},... | collective-permute-start | bytes 614408 | tf_op jit(solution)/shard_map/ppermute | solution.py:211
  62.1 2.0 %collective-permute-done.2.refs_0_.refs_3_ = bf16[80,1280]{1,0:T(8,128)(2,1)S(1)} collective-permute-done((bf16[80,1280]{1,0:T(8,128)(2,1)S(1)}, bf16[80,1280]{1,0:T(8,128)(2,1)S(1)}, u32[]{:S(2)}, u32[]{:S(2)}) %collective-permute-start.2) | collective-permute-done | bytes 204832 | tf_op jit(solution)/shard_map/ppermute | solution.py:214
  64.1 4.9 %collective-permute-done.6.refs_2_.refs_4_ = bf16[80,1280]{1,0:T(8,128)(2,1)S(1)} collective-permute-done((bf16[80,1280]{1,0:T(8,128)(2,1)S(1)}, bf16[80,1280]{1,0:T(8,128)(2,1)S(1)}, u32[]{:S(2)}, u32[]{:S(2)}) %collective-permute-start.6) | collective-permute-done | bytes 204832 | tf_op jit(solution)/shard_map/ppermute | solution.py:211
  69.0 1.9 %collective-permute-start.8 = (bf16[3,80,1280]{2,1,0:T(8,128)(2,1)S(1)}, bf16[3,80,1280]{2,1,0:T(8,128)(2,1)S(1)}, u32[]{:S(2)}, u32[]{:S(2)}) collective-permute-start(bf16[3,80,1280]{2,1,0:T(8,128)(2,1)S(1)} %shard_map.75), channel_id=1, source_target_pairs={{0,64},{64,0},{128,192},{192,128},{256,320},{320,256},{384,448},{4... | collective-permute-start | bytes 1843208 | tf_op jit(solution)/shard_map/ppermute | solution.py:218
  71.0 2.0 %collective-permute-done.8.refs_9_ = bf16[3,80,1280]{2,1,0:T(8,128)(2,1)S(1)} collective-permute-done((bf16[3,80,1280]{2,1,0:T(8,128)(2,1)S(1)}, bf16[3,80,1280]{2,1,0:T(8,128)(2,1)S(1)}, u32[]{:S(2)}, u32[]{:S(2)}) %collective-permute-start.8) | collective-permute-done | bytes 614432 | tf_op jit(solution)/shard_map/ppermute | solution.py:218
  73.0 5.5 %shard_map.76 = (bf16[1280,1280]{1,0:T(8,128)(2,1)}, bf16[512,640]{1,0:T(8,128)(2,1)}) custom-call(s32[1,4]{1,0:T(1,128)S(1)} %copy-done.5, bf16[80,1280]{1,0:T(8,128)(2,1)S(1)} %bitcast.11, bf16[80,1280]{1,0:T(8,128)(2,1)S(1)} %collective-permute-done.refs_1_, bf16[80,1280]{1,0:T(8,128)(2,1)S(1)} %collective-permute-done.1.refs_3_.refs_2_, ...), custom_call_target="tpu_custom_call" | custom-call | flops 629145600 | bytes 1048576 | tf_op jit(solution)/shard_map/pallas_call | solution.py:32
  78.5 0.0 all-to-all-done
  78.5 12.7 %all-to-all-start.1 = ((bf16[64,8,640]{2,1,0:T(8,128)(2,1)}), bf16[64,8,640]{2,1,0:T(8,128)(2,1)S(1)}, u32[]{:S(2)}, u32[]{:S(2)}) async-start(bf16[64,8,640]{2,1,0:T(8,128)(2,1)} %bitcast.4), calls=%async_computation.1 | async-start | bytes 1310720 | tf_op jit(solution)/shard_map/all_to_all | solution.py:257
  91.2 1.9 %copy-done.7 = bf16[1280,1280]{1,0:T(8,128)(2,1)S(1)} copy-done((bf16[1280,1280]{1,0:T(8,128)(2,1)S(1)}, bf16[1280,1280]{1,0:T(8,128)(2,1)}, u32[]{:S(2)}) %copy-start.7) | copy-done | bytes 3276824
  93.2 2.7 %shard_map.77.first_ref = bf16[128,5120]{1,0:T(8,128)(2,1)S(1)} custom-call(bf16[512,1280]{1,0:T(8,128)(2,1)S(1)} %bitcast.7, bf16[1280,1280]{1,0:T(8,128)(2,1)S(1)} %copy-done.7, f32[1280]{0:T(1024)S(1)} %copy-done.3, f32[1280]{0:T(1024)S(1)} %copy-done.4), custom_call_target="tpu_custom_call" | custom-call | flops 2147483648 | bytes 1048576 | tf_op jit(solution)/shard_map/pallas_call | solution.py:32
  95.9 17.8 %all-to-all-done.1 = bf16[64,8,640]{2,1,0:T(8,128)(2,1)S(1)} async-done(((bf16[64,8,640]{2,1,0:T(8,128)(2,1)}), bf16[64,8,640]{2,1,0:T(8,128)(2,1)S(1)}, u32[]{:S(2)}, u32[]{:S(2)}) %all-to-all-start.1) | async-done | bytes 655392 | tf_op jit(solution)/shard_map/all_to_all | solution.py:257
  113.7 1.9 %shard_map.78 = bf16[128,5120]{1,0:T(8,128)(2,1)} custom-call(bf16[128,5120]{1,0:T(8,128)(2,1)S(1)} %shard_map.77.first_ref, bf16[512,640]{1,0:T(8,128)(2,1)S(1)} %bitcast.6), custom_call_target="tpu_custom_call" | custom-call | flops 536870912 | bytes 1048576 | tf_op jit(solution)/shard_map/pallas_call | solution.py:32
  (12 shorter events, 0.1 us)
Async XLA Ops:
  5.9 17.5 %copy-start = (bf16[1280,80]{0,1:T(8,128)(2,1)S(1)}, bf16[1280,80]{0,1:T(8,128)(2,1)}, u32[]{:S(2)}) copy-start(bf16[1280,80]{0,1:T(8,128)(2,1)} %param.11) | copy-start | bytes 614404
  5.9 72.6 %all-to-all-start = ((bf16[64,8,1280]{2,1,0:T(8,128)(2,1)}), bf16[64,8,1280]{2,1,0:T(8,128)(2,1)S(1)}, u32[]{:S(2)}, u32[]{:S(2)}) async-start(bf16[64,8,1280]{2,1,0:T(8,128)(2,1)} %bitcast.1), calls=%async_computation | async-start | bytes 2621440 | tf_op jit(solution)/shard_map/all_to_all | solution.py:247
  23.4 49.6 %copy-start.1 = (bf16[192,1280]{1,0:T(8,128)(2,1)S(1)}, bf16[192,1280]{1,0:T(8,128)(2,1)}, u32[]{:S(2)}) copy-start(bf16[192,1280]{1,0:T(8,128)(2,1)} %refs_12_.1) | copy-start | bytes 1474564
  23.4 49.6 %copy-start.2 = (bf16[192,1280]{1,0:T(8,128)(2,1)S(1)}, bf16[192,1280]{1,0:T(8,128)(2,1)}, u32[]{:S(2)}) copy-start(bf16[192,1280]{1,0:T(8,128)(2,1)} %get-tuple-element.10.refs_11_) | copy-start | bytes 1474564
  23.4 49.6 %copy-start.3 = (f32[1280]{0:T(1024)S(1)}, f32[1280]{0:T(1024)}, u32[]{:S(2)}) copy-start(f32[1280]{0:T(1024)} %gain_ref.1) | copy-start | bytes 15364
  23.4 49.6 %copy-start.4 = (f32[1280]{0:T(1024)S(1)}, f32[1280]{0:T(1024)}, u32[]{:S(2)}) copy-start(f32[1280]{0:T(1024)} %bias_ref.1) | copy-start | bytes 15364
  23.4 49.6 %copy-start.5 = (s32[1,4]{1,0:T(1,128)S(1)}, s32[1,4]{1,0:T(1,128)}, u32[]{:S(2)}) copy-start(s32[1,4]{1,0:T(1,128)} %counts_ref.1) | copy-start | bytes 52
  23.4 49.6 %copy-start.6 = (s32[48,1]{0,1:T(1,128)S(1)}, s32[48,1]{0,1:T(1,128)}, u32[]{:S(2)}) copy-start(s32[48,1]{0,1:T(1,128)} %param.10) | copy-start | bytes 580
  23.5 17.4 %collective-permute-start.3 = (bf16[80,1280]{1,0:T(8,128)(2,1)S(1)}, bf16[80,1280]{1,0:T(8,128)(2,1)S(1)}, u32[]{:S(2)}, u32[]{:S(2)}) collective-permute-start(bf16[80,1280]{1,0:T(8,128)(2,1)S(1)} %bitcast.8), channel_id=1, source_target_pairs={{0,128},{64,960},{128,256},{192,64},{256,384},{320,192},{384,512},... | collective-permute-start | bytes 614408 | tf_op jit(solution)/shard_map/ppermute | solution.py:211
  25.5 17.2 %collective-permute-start = (bf16[80,1280]{1,0:T(8,128)(2,1)S(1)}, bf16[80,1280]{1,0:T(8,128)(2,1)S(1)}, u32[]{:S(2)}, u32[]{:S(2)}) collective-permute-start(bf16[80,1280]{1,0:T(8,128)(2,1)S(1)} %bitcast.9), channel_id=1, source_target_pairs={{128,0},{960,64},{256,128},{64,192},{384,256},{192,320},{512,384},... | collective-permute-start | bytes 614408 | tf_op jit(solution)/shard_map/ppermute | solution.py:214
  40.8 10.2 %collective-permute-start.4 = (bf16[80,1280]{1,0:T(8,128)(2,1)S(1)}, bf16[80,1280]{1,0:T(8,128)(2,1)S(1)}, u32[]{:S(2)}, u32[]{:S(2)}) collective-permute-start(bf16[80,1280]{1,0:T(8,128)(2,1)S(1)} %collective-permute-done.3.refs_2_.refs_7_), channel_id=1, source_target_pairs={{0,128},{64,960},{128,256},{192,64},{256,384},{320,192},{384,512},... | collective-permute-start | bytes 614408 | tf_op jit(solution)/shard_map/ppermute | solution.py:211
  42.8 10.2 %collective-permute-start.1 = (bf16[80,1280]{1,0:T(8,128)(2,1)S(1)}, bf16[80,1280]{1,0:T(8,128)(2,1)S(1)}, u32[]{:S(2)}, u32[]{:S(2)}) collective-permute-start(bf16[80,1280]{1,0:T(8,128)(2,1)S(1)} %collective-permute-done.refs_1_), channel_id=1, source_target_pairs={{128,0},{960,64},{256,128},{64,192},{384,256},{192,320},{512,384},... | collective-permute-start | bytes 614408 | tf_op jit(solution)/shard_map/ppermute | solution.py:214
  51.0 9.1 %collective-permute-start.5 = (bf16[80,1280]{1,0:T(8,128)(2,1)S(1)}, bf16[80,1280]{1,0:T(8,128)(2,1)S(1)}, u32[]{:S(2)}, u32[]{:S(2)}) collective-permute-start(bf16[80,1280]{1,0:T(8,128)(2,1)S(1)} %collective-permute-done.4.refs_4_.refs_6_), channel_id=1, source_target_pairs={{0,128},{64,960},{128,256},{192,64},{256,384},{320,192},{384,512},... | collective-permute-start | bytes 614408 | tf_op jit(solution)/shard_map/ppermute | solution.py:211
  53.1 19.9 %collective-permute-start.7 = (bf16[5,80,1280]{2,1,0:T(8,128)(2,1)S(1)}, bf16[5,80,1280]{2,1,0:T(8,128)(2,1)S(1)}, u32[]{:S(2)}, u32[]{:S(2)}) collective-permute-start(bf16[5,80,1280]{2,1,0:T(8,128)(2,1)S(1)} %shard_map.74), channel_id=1, source_target_pairs={{0,64},{64,0},{128,192},{192,128},{256,320},{320,256},{384,448},{4... | collective-permute-start | bytes 3072008 | tf_op jit(solution)/shard_map/ppermute | solution.py:218
  55.0 9.1 %collective-permute-start.2 = (bf16[80,1280]{1,0:T(8,128)(2,1)S(1)}, bf16[80,1280]{1,0:T(8,128)(2,1)S(1)}, u32[]{:S(2)}, u32[]{:S(2)}) collective-permute-start(bf16[80,1280]{1,0:T(8,128)(2,1)S(1)} %collective-permute-done.1.refs_3_.refs_2_), channel_id=1, source_target_pairs={{128,0},{960,64},{256,128},{64,192},{384,256},{192,320},{512,384},... | collective-permute-start | bytes 614408 | tf_op jit(solution)/shard_map/ppermute | solution.py:214
  60.1 8.9 %collective-permute-start.6 = (bf16[80,1280]{1,0:T(8,128)(2,1)S(1)}, bf16[80,1280]{1,0:T(8,128)(2,1)S(1)}, u32[]{:S(2)}, u32[]{:S(2)}) collective-permute-start(bf16[80,1280]{1,0:T(8,128)(2,1)S(1)} %collective-permute-done.5.refs_1_.refs_5_), channel_id=1, source_target_pairs={{0,128},{64,960},{128,256},{192,64},{256,384},{320,192},{384,512},... | collective-permute-start | bytes 614408 | tf_op jit(solution)/shard_map/ppermute | solution.py:211
  69.0 3.9 %collective-permute-start.8 = (bf16[3,80,1280]{2,1,0:T(8,128)(2,1)S(1)}, bf16[3,80,1280]{2,1,0:T(8,128)(2,1)S(1)}, u32[]{:S(2)}, u32[]{:S(2)}) collective-permute-start(bf16[3,80,1280]{2,1,0:T(8,128)(2,1)S(1)} %shard_map.75), channel_id=1, source_target_pairs={{0,64},{64,0},{128,192},{192,128},{256,320},{320,256},{384,448},{4... | collective-permute-start | bytes 1843208 | tf_op jit(solution)/shard_map/ppermute | solution.py:218
  78.5 35.2 %all-to-all-start.1 = ((bf16[64,8,640]{2,1,0:T(8,128)(2,1)}), bf16[64,8,640]{2,1,0:T(8,128)(2,1)S(1)}, u32[]{:S(2)}, u32[]{:S(2)}) async-start(bf16[64,8,640]{2,1,0:T(8,128)(2,1)} %bitcast.4), calls=%async_computation.1 | async-start | bytes 1310720 | tf_op jit(solution)/shard_map/all_to_all | solution.py:257
  91.2 1.9 %copy-start.7 = (bf16[1280,1280]{1,0:T(8,128)(2,1)S(1)}, bf16[1280,1280]{1,0:T(8,128)(2,1)}, u32[]{:S(2)}) copy-start(bf16[1280,1280]{1,0:T(8,128)(2,1)} %get-tuple-element.11.weight_ref) | copy-start | bytes 9830404

commit v3 on v2

--- a/solution.py
+++ b/solution.py
@@ -6,7 +6,6 @@
 from jax.experimental import pallas as pl
 from jax.experimental.pallas import tpu as pltpu
 from jax.sharding import PartitionSpec as P
-
 
 HEADS = 16
 IMGS = 4
@@ -62,19 +61,29 @@
 
 
 def front_kernel(
-    counts_in, owner_in, packed_in, patch_in, context_out, send_ref,
-    counts_ref, owner_ref, packed_ref, patch_ref, context_ref, done
+    counts_in, owner_in, packed_in, patch_in, send_out,
+    counts_ref, owner_ref, packed_ref, patch_ref, context_ref, send_ref, done, left
 ):
     rows, width = patch_ref.shape
     head_size = width // HEADS
-    pairs = ((counts_in, counts_ref), (packed_in, packed_ref), (owner_in, owner_ref), (patch_in, patch_ref))
+    pairs = ((counts_in, counts_ref), (owner_in, owner_ref), (patch_in, patch_ref), (packed_in, packed_ref))
     fetches = [pltpu.make_async_copy(src, dst, done.at[i]) for i, (src, dst) in enumerate(pairs)]
     for fetch in fetches:
         fetch.start()
     context_ref[...] = jnp.zeros_like(context_ref)
-    fetches[0].wait()
-    fetches[1].wait()
+    for fetch in fetches[:3]:
+        fetch.wait()
     ends = image_ends(counts_ref)
+    owner_row, slot, live, part = row_slots(ends, owner_ref, rows)
+    key = jnp.where(live, owner_row * 8 + slot.astype(jnp.int32) * 4 + part, DEAD)
+    lines = send_ref.shape[0]
+    hits = key == iota((lines, 1), 0)
+    held = jnp.sum(jnp.where(hits, 1.0, 0.0), axis=1, keepdims=True)
+    marker = jnp.where(held == 0.0, 64.0, 0.0)
+    send_ref[:, :width] = (pick(hits, patch_ref[...]) + marker).astype(BF16)
+    leaves = [pltpu.make_async_copy(send_ref.at[:, :width], send_out.at[:, :width], left.at[4])]
+    leaves[0].start()
+    fetches[3].wait()
     lane, sub = iota((1, rows), 1), iota((rows, 1), 0)
     segment_row = sum((lane >= end).astype(jnp.int32) for end in ends)
     segment_col = sum((sub >= end).astype(jnp.int32) for end in ends)
@@ -96,19 +105,15 @@
         values = packed_ref[:, 2 * width + start : 2 * width + start + 256]
         mixed = jnp.dot(weights, values, preferred_element_type=F32).astype(BF16)
         context_ref[:, start : start + 256] = jnp.where(mine, mixed, context_ref[:, start : start + 256])
-    leave = pltpu.make_async_copy(context_ref, context_out, done.at[4])
-    leave.start()
-    fetches[2].wait()
-    fetches[3].wait()
-    owner_row, slot, live, part = row_slots(ends, owner_ref, rows)
-    key = jnp.where(live & (slot == 0.0), owner_row * 8 + part, DEAD)
-    line = iota((send_ref.shape[0], 1), 0)
-    hits = key == line
-    held = jnp.sum(jnp.where(hits, 1.0, 0.0), axis=1, keepdims=True)
-    marker = jnp.where((held == 0.0) & ((line & 7) < 4), 64.0, 0.0)
-    sent = pick(hits, patch_ref[...]) + pick(key == line - 4, context_ref[...]) + marker
-    send_ref[...] = sent.astype(BF16)
-    leave.wait()
+    for i in range(4):
+        place = slice(i * lines // 4, (i + 1) * lines // 4)
+        wanted = iota((lines // 4, 1), 0) + i * lines // 4
+        send_ref[place, width:] = pick(key == wanted, context_ref[...]).astype(BF16)
+        leave = pltpu.make_async_copy(send_ref.at[place, width:], send_out.at[place, width:], left.at[i])
+        leave.start()
+        leaves.append(leave)
+    for leave in leaves:
+        leave.wait()
 
 
 def norm(hidden, gain, bias):
@@ -123,65 +128,52 @@
     return lax.dot_general(context, weight, (((1,), (1,)), ((), ())), preferred_element_type=F32)
 
 
-def late_kernel(nz, splits, counts_ref, *refs):
-    blocks, refs = refs[:nz], refs[nz:]
-    halves, refs = refs[: len(splits)], refs[len(splits) :]
-    owner_ref, context_ref, patch_ref, gain_ref, bias_ref = refs[:5]
-    weight_out, send_ref, weight_ref, done = refs[5:]
+def gather_kernel(nz, splits, *refs):
+    blocks, halves, (weight_out, done) = refs[:nz], refs[nz : nz + len(splits)], refs[nz + len(splits) :]
     block_width = blocks[0].shape[0]
     me = lax.axis_index("dp")
     z, c = lax.shift_right_logical(me, 1), lax.bitwise_and(me, 1)
     pieces = [(j, c, blocks[j]) for j in range(nz)]
     for part, ref in zip(splits, halves):
         pieces += [(j, 1 - c, ref.at[i]) for i, j in enumerate(part)]
-    leaves, places = [], []
+    leaves = []
     for i, (j, core, ref) in enumerate(pieces):
         owner = lax.rem(z + j * (1 - 2 * core) + nz, nz) * 2 + core
-        places.append(pl.ds(pl.multiple_of(owner * block_width, 16), block_width))
-        leaves.append(pltpu.make_async_copy(ref, weight_out.at[places[i], :], done.at[i]))
+        place = pl.ds(pl.multiple_of(owner * block_width, 16), block_width)
+        leaves.append(pltpu.make_async_copy(ref, weight_out.at[place, :], done.at[i]))
         leaves[i].start()
-    for place, (_, _, ref) in zip(places, pieces):
-        weight_ref[place, :] = ref[...]
-    hidden = patch_ref[...].astype(F32) + project(context_ref[...], weight_ref[...])
-    normed = norm(hidden, gain_ref[...], bias_ref[...]).astype(BF16)
-    owner_row, slot, live, part = row_slots(image_ends(counts_ref), owner_ref, patch_ref.shape[0])
-    key = jnp.where(live & (slot == 1.0), owner_row * 8 + 2 * part, DEAD)
-    line = iota((send_ref.shape[0], 1), 0)
-    half = send_ref.shape[1]
-    sent = pick(key == line, normed[:, :half]) + pick(key == line - 1, normed[:, half:])
-    send_ref[...] = sent.astype(BF16)
     for leave in leaves:
         leave.wait()
 
 
-def early_kernel(received_ref, weight_ref, gain_ref, bias_ref, out_ref):
-    lines, width = received_ref.shape
-    owners = lines // 8
-    row = iota((4 * owners, 1), 0)
-    place = (row & (owners - 1)) * 8 + (row >> (owners.bit_length() - 1))
-    column = iota((1, lines), 1)
-    patches = pick(column == place, received_ref[...])
-    context = pick(column == place + 4, received_ref[...]).astype(BF16)
-    normed = norm(patches + project(context, weight_ref[...]), gain_ref[...], bias_ref[...])
-    normed = jnp.where(patches[:, :1] > 32.0, 0.0, normed).astype(BF16)
-    even = iota((2 * owners, 1), 0) == 2 * iota((1, owners), 1)
-    for part in range(4):
-        first = pick(even, normed[part * owners : (part + 1) * owners, :])
-        out_ref[:, part * width : (part + 1) * width] = first.astype(BF16)
-
-
-def join_kernel(first_ref, received_ref, out_ref, joined_ref, done):
-    lines, half = received_ref.shape
-    slots = lines // 4
-    row = iota((8 * slots, 1), 0)
-    slot, chunk = row & (slots - 1), row >> (slots.bit_length() - 1)
-    hits = (iota((1, lines), 1) == 4 * (slot - 1) + chunk) & ((slot & 1) == 1)
-    second = pick(hits, received_ref[...]).astype(BF16)
+def finish_kernel(weight_in, received_ref, gain_ref, bias_ref, out_ref, weight_ref, hidden_ref, joined_ref, done):
+    lines, width = hidden_ref.shape
+    step = 256
+    fetches = []
+    for i in range(width // step):
+        part = slice(i * step, (i + 1) * step)
+        fetches.append(pltpu.make_async_copy(weight_in.at[part, :], weight_ref.at[part, :], done.at[i]))
+        fetches[i].start()
+    for i, fetch in enumerate(fetches):
+        fetch.wait()
+        part = slice(i * step, (i + 1) * step)
+        patches = received_ref[:, part].astype(F32)
+        hidden_ref[:, part] = patches + project(received_ref[:, width:], weight_ref[part, :])
     leaves = []
-    for i in range(8):
-        columns = slice(i * half, (i + 1) * half)
-        joined_ref[:, columns] = first_ref[:, columns] + second[i * slots : (i + 1) * slots]
-        leave = pltpu.make_async_copy(joined_ref.at[:, columns], out_ref.at[:, columns], done.at[i])
+    chunk = min(256, lines)
+    slots = chunk // 4
+    row = iota((chunk, 1), 0)
+    wanted = (row & (slots - 1)) * 4 + (row >> (slots.bit_length() - 1))
+    hits = iota((1, chunk), 1) == wanted
+    for i in range(lines // chunk):
+        part = slice(i * chunk, (i + 1) * chunk)
+        normed = norm(hidden_ref[part, :], gain_ref[...], bias_ref[...])
+        normed = jnp.where(received_ref[part, :1].astype(F32) > 32.0, 0.0, normed).astype(BF16)
+        joined = pick(hits, normed).astype(BF16)
+        place = slice(i * slots, (i + 1) * slots)
+        for k in range(4):
+            joined_ref[place, k * width : (k + 1) * width] = joined[k * slots : (k + 1) * slots]
+        leave = pltpu.make_async_copy(joined_ref.at[place, :], out_ref.at[place, :], done.at[8 + i])
         leave.start()
         leaves.append(leave)
     for leave in leaves:
@@ -227,9 +219,9 @@
     lines = 8 * owners
 
     blocks, splits, halves = ring_gather(out_weight.T)
-    context, send = call(
+    send = call(
         front_kernel,
-        (pltpu.HBM((rows, width), BF16), jax.ShapeDtypeStruct((lines, width), BF16)),
+        pltpu.HBM((lines, 2 * width), BF16),
         [pltpu.with_memory_space_constraint(x, pltpu.HBM) for x in (counts, owner_lanes, query_key_value, patches)],
         1 << 31,
         scratch=[
@@ -238,32 +230,37 @@
             pltpu.VMEM((rows, 3 * width), BF16),
             pltpu.VMEM((rows, width), BF16),
             pltpu.VMEM((rows, width), BF16),
+            pltpu.VMEM((lines, 2 * width), BF16),
+            pltpu.SemaphoreType.DMA((4,)),
             pltpu.SemaphoreType.DMA((5,)),
         ],
-        out_specs=(HBM, VMEM),
         in_specs=[HBM] * 4,
+        out_specs=HBM,
         limit=16,
     )
     received = lax.all_to_all(send, "seq", split_axis=0, concat_axis=0, tiled=True)
-    weight, late_send = call(
-        functools.partial(late_kernel, nz, splits),
-        (pltpu.HBM((width, width), BF16), jax.ShapeDtypeStruct((lines, width // 2), BF16)),
-        [counts, *blocks, *halves, owner_lanes, context, patches, ln_gain, ln_bias],
-        2 * rows * width * width,
-        scratch=[pltpu.VMEM((width, width), BF16), pltpu.SemaphoreType.DMA((2 * nz,))],
-        smem=1,
-        out_specs=(HBM, VMEM),
-    )
-    late_received = lax.all_to_all(late_send, "seq", split_axis=0, concat_axis=0, tiled=True)
-    shape = jax.ShapeDtypeStruct((2 * owners, 4 * width), BF16)
-    first = call(early_kernel, shape, [received, weight, ln_gain, ln_bias], 1 << 31)
+    weight = call(
+        functools.partial(gather_kernel, nz, splits),
+        pltpu.HBM((width, width), BF16),
+        [*blocks, *halves],
+        1 << 28,
+        scratch=[pltpu.SemaphoreType.DMA((2 * nz,))],
+        out_specs=HBM,
+    )
     return call(
-        join_kernel,
-        pltpu.HBM(shape.shape, BF16),
-        [first, late_received],
-        1 << 29,
-        scratch=[pltpu.VMEM(shape.shape, BF16), pltpu.SemaphoreType.DMA((8,))],
+        finish_kernel,
+        pltpu.HBM((2 * owners, 4 * width), BF16),
+        [pltpu.with_memory_space_constraint(weight, pltpu.HBM), received, ln_gain, ln_bias],
+        1 << 31,
+        scratch=[
+            pltpu.VMEM((width, width), BF16),
+            pltpu.VMEM((lines, width), F32),
+            pltpu.VMEM((2 * owners, 4 * width), BF16),
+            pltpu.SemaphoreType.DMA((16,)),
+        ],
+        in_specs=[HBM, VMEM, VMEM, VMEM],
         out_specs=HBM,
+        limit=24,
     )
 
 

time: 116 us -> 96.7 us (0.83)
  the two profiles are of different devices: /device:TPU:4 before, /device:TPU:638 now
where the time goes in v3:
time: 96.7 us; the launch traced here: 96.2 us
  waiting for transfers between devices  42.8 us (44%)
  starting transfers between devices  38.2 us (40%)
  Pallas kernels  15 us (16%)
    all_to_all x1, waiting for transfers between devices, step(): lax.all_to_all(send, 'seq', split_axis=0, concat_axis=0, tiled=True)  25.8 us
    pallas_call x5, Pallas kernels, call(): pl.pallas_call(kernel, out_shape=out_shape, in_specs=in_specs or [SMEM] *...  15 us
    ppermute x4, waiting for transfers between devices, ring_gather(): from_below = lax.ppermute(from_below, 'dp', up)  12.3 us
    all_to_all x1, starting transfers between devices, step(): lax.all_to_all(send, 'seq', split_axis=0, concat_axis=0, tiled=True)  12.3 us
    ppermute x4, starting transfers between devices, ring_gather(): from_below = lax.ppermute(from_below, 'dp', up)  11.2 us
    ppermute x3, starting transfers between devices, ring_gather(): from_above = lax.ppermute(from_above, 'dp', down)  10.9 us
    ppermute x2, starting transfers between devices, ring_gather(): lax.ppermute(pack([blocks[j] for j in part]), 'dp', swap)  3.84 us
    ppermute x3, waiting for transfers between devices, ring_gather(): from_above = lax.ppermute(from_above, 'dp', down)  2.71 us
  transfers between devices with their start and end apart: 10, of which 7 were waited for; matrix products, arithmetic and copies ran while one was open for 0% of the time, Pallas kernels for 2%

profile of v3, /device:TPU:638, one launch (start us, length us, event | category | flops | bytes accessed | tf_op | source)
XLA Modules:
  0.0 96.2 jit_solution(14165188166053586314)
XLA Ops:
  0.0 5.4 %shard_map.76 = bf16[512,2560]{1,0:T(8,128)(2,1)} custom-call(s32[1,4]{1,0:T(1,128)} %counts_in.1, s32[1,48]{1,0:T(1,128)} %bitcast.10, bf16[192,3840]{1,0:T(8,128)(2,1)} %packed_in.1, bf16[192,1280]{1,0:T(8,128)(2,1)} %patch_in.1), custom_call_target="tpu_custom_call" | custom-call | flops 2147483648 | bytes 1048576 | tf_op jit(solution)/shard_map/pallas_call | solution.py:31
  5.5 0.0 copy-start
  5.5 12.3 %all-to-all-start = ((bf16[64,8,2560]{2,1,0:T(8,128)(2,1)}), bf16[64,8,2560]{2,1,0:T(8,128)(2,1)S(1)}, u32[]{:S(2)}, u32[]{:S(2)}) async-start(bf16[64,8,2560]{2,1,0:T(8,128)(2,1)} %bitcast.9), calls=%async_computation | async-start | bytes 5242880 | tf_op jit(solution)/shard_map/all_to_all | solution.py:241
  17.7 0.0 copy-done
  17.7 4.3 %collective-permute-start.3 = (bf16[80,1280]{1,0:T(8,128)(2,1)S(1)}, bf16[80,1280]{1,0:T(8,128)(2,1)S(1)}, u32[]{:S(2)}, u32[]{:S(2)}) collective-permute-start(bf16[80,1280]{1,0:T(8,128)(2,1)S(1)} %bitcast.5), channel_id=1, source_target_pairs={{0,128},{64,960},{128,256},{192,64},{256,384},{320,192},{384,512},... | collective-permute-start | bytes 614408 | tf_op jit(solution)/shard_map/ppermute | solution.py:203
  22.0 2.8 %collective-permute-start = (bf16[80,1280]{1,0:T(8,128)(2,1)S(1)}, bf16[80,1280]{1,0:T(8,128)(2,1)S(1)}, u32[]{:S(2)}, u32[]{:S(2)}) collective-permute-start(bf16[80,1280]{1,0:T(8,128)(2,1)S(1)} %bitcast.6), channel_id=1, source_target_pairs={{128,0},{960,64},{256,128},{64,192},{384,256},{192,320},{512,384},... | collective-permute-start | bytes 614408 | tf_op jit(solution)/shard_map/ppermute | solution.py:206
  24.8 3.8 %collective-permute-done.3.refs_2_.refs_7_ = bf16[80,1280]{1,0:T(8,128)(2,1)S(1)} collective-permute-done((bf16[80,1280]{1,0:T(8,128)(2,1)S(1)}, bf16[80,1280]{1,0:T(8,128)(2,1)S(1)}, u32[]{:S(2)}, u32[]{:S(2)}) %collective-permute-start.3) | collective-permute-done | bytes 204832 | tf_op jit(solution)/shard_map/ppermute | solution.py:203
  28.6 3.1 %collective-permute-start.4 = (bf16[80,1280]{1,0:T(8,128)(2,1)S(1)}, bf16[80,1280]{1,0:T(8,128)(2,1)S(1)}, u32[]{:S(2)}, u32[]{:S(2)}) collective-permute-start(bf16[80,1280]{1,0:T(8,128)(2,1)S(1)} %collective-permute-done.3.refs_2_.refs_7_), channel_id=1, source_target_pairs={{0,128},{64,960},{128,256},{192,64},{256,384},{320,192},{384,512},... | collective-permute-start | bytes 614408 | tf_op jit(solution)/shard_map/ppermute | solution.py:203
  31.6 0.0 collective-permute-done.refs_1_
  31.7 4.0 %collective-permute-start.1 = (bf16[80,1280]{1,0:T(8,128)(2,1)S(1)}, bf16[80,1280]{1,0:T(8,128)(2,1)S(1)}, u32[]{:S(2)}, u32[]{:S(2)}) collective-permute-start(bf16[80,1280]{1,0:T(8,128)(2,1)S(1)} %collective-permute-done.refs_1_), channel_id=1, source_target_pairs={{128,0},{960,64},{256,128},{64,192},{384,256},{192,320},{512,384},... | collective-permute-start | bytes 614408 | tf_op jit(solution)/shard_map/ppermute | solution.py:206
  35.6 3.4 %collective-permute-done.4.refs_4_.refs_6_ = bf16[80,1280]{1,0:T(8,128)(2,1)S(1)} collective-permute-done((bf16[80,1280]{1,0:T(8,128)(2,1)S(1)}, bf16[80,1280]{1,0:T(8,128)(2,1)S(1)}, u32[]{:S(2)}, u32[]{:S(2)}) %collective-permute-start.4) | collective-permute-done | bytes 204832 | tf_op jit(solution)/shard_map/ppermute | solution.py:203
  39.0 1.9 %collective-permute-start.5 = (bf16[80,1280]{1,0:T(8,128)(2,1)S(1)}, bf16[80,1280]{1,0:T(8,128)(2,1)S(1)}, u32[]{:S(2)}, u32[]{:S(2)}) collective-permute-start(bf16[80,1280]{1,0:T(8,128)(2,1)S(1)} %collective-permute-done.4.refs_4_.refs_6_), channel_id=1, source_target_pairs={{0,128},{64,960},{128,256},{192,64},{256,384},{320,192},{384,512},... | collective-permute-start | bytes 614408 | tf_op jit(solution)/shard_map/ppermute | solution.py:203
  40.9 0.9 collective-permute-done.1.refs_3_.refs_2_
  41.8 0.1 shard_map.73
  41.9 1.9 %collective-permute-start.7 = (bf16[5,80,1280]{2,1,0:T(8,128)(2,1)S(1)}, bf16[5,80,1280]{2,1,0:T(8,128)(2,1)S(1)}, u32[]{:S(2)}, u32[]{:S(2)}) collective-permute-start(bf16[5,80,1280]{2,1,0:T(8,128)(2,1)S(1)} %shard_map.73), channel_id=1, source_target_pairs={{0,64},{64,0},{128,192},{192,128},{256,320},{320,256},{384,448},{4... | collective-permute-start | bytes 3072008 | tf_op jit(solution)/shard_map/ppermute | solution.py:210
  43.8 4.2 %collective-permute-start.2 = (bf16[80,1280]{1,0:T(8,128)(2,1)S(1)}, bf16[80,1280]{1,0:T(8,128)(2,1)S(1)}, u32[]{:S(2)}, u32[]{:S(2)}) collective-permute-start(bf16[80,1280]{1,0:T(8,128)(2,1)S(1)} %collective-permute-done.1.refs_3_.refs_2_), channel_id=1, source_target_pairs={{128,0},{960,64},{256,128},{64,192},{384,256},{192,320},{512,384},... | collective-permute-start | bytes 614408 | tf_op jit(solution)/shard_map/ppermute | solution.py:206
  48.1 0.0 collective-permute-done.5.refs_1_.refs_5_
  48.1 1.9 %collective-permute-start.6 = (bf16[80,1280]{1,0:T(8,128)(2,1)S(1)}, bf16[80,1280]{1,0:T(8,128)(2,1)S(1)}, u32[]{:S(2)}, u32[]{:S(2)}) collective-permute-start(bf16[80,1280]{1,0:T(8,128)(2,1)S(1)} %collective-permute-done.5.refs_1_.refs_5_), channel_id=1, source_target_pairs={{0,128},{64,960},{128,256},{192,64},{256,384},{320,192},{384,512},... | collective-permute-start | bytes 614408 | tf_op jit(solution)/shard_map/ppermute | solution.py:203
  50.0 1.8 %collective-permute-done.2.refs_0_.refs_3_ = bf16[80,1280]{1,0:T(8,128)(2,1)S(1)} collective-permute-done((bf16[80,1280]{1,0:T(8,128)(2,1)S(1)}, bf16[80,1280]{1,0:T(8,128)(2,1)S(1)}, u32[]{:S(2)}, u32[]{:S(2)}) %collective-permute-start.2) | collective-permute-done | bytes 204832 | tf_op jit(solution)/shard_map/ppermute | solution.py:206
  51.8 5.2 %collective-permute-done.6.refs_2_.refs_4_ = bf16[80,1280]{1,0:T(8,128)(2,1)S(1)} collective-permute-done((bf16[80,1280]{1,0:T(8,128)(2,1)S(1)}, bf16[80,1280]{1,0:T(8,128)(2,1)S(1)}, u32[]{:S(2)}, u32[]{:S(2)}) %collective-permute-start.6) | collective-permute-done | bytes 204832 | tf_op jit(solution)/shard_map/ppermute | solution.py:203
  57.0 0.0 copy-start.1
  57.0 0.0 copy-start.2
  57.0 1.9 %collective-permute-start.8 = (bf16[3,80,1280]{2,1,0:T(8,128)(2,1)S(1)}, bf16[3,80,1280]{2,1,0:T(8,128)(2,1)S(1)}, u32[]{:S(2)}, u32[]{:S(2)}) collective-permute-start(bf16[3,80,1280]{2,1,0:T(8,128)(2,1)S(1)} %shard_map.74), channel_id=1, source_target_pairs={{0,64},{64,0},{128,192},{192,128},{256,320},{320,256},{384,448},{4... | collective-permute-start | bytes 1843208 | tf_op jit(solution)/shard_map/ppermute | solution.py:210
  58.9 2.0 %collective-permute-done.8.refs_9_ = bf16[3,80,1280]{2,1,0:T(8,128)(2,1)S(1)} collective-permute-done((bf16[3,80,1280]{2,1,0:T(8,128)(2,1)S(1)}, bf16[3,80,1280]{2,1,0:T(8,128)(2,1)S(1)}, u32[]{:S(2)}, u32[]{:S(2)}) %collective-permute-start.8) | collective-permute-done | bytes 614432 | tf_op jit(solution)/shard_map/ppermute | solution.py:210
  60.9 0.0 collective-permute-done.7.refs_8_
  60.9 1.9 %shard_map.75.weight_in = bf16[1280,1280]{1,0:T(8,128)(2,1)} custom-call(bf16[80,1280]{1,0:T(8,128)(2,1)S(1)} %bitcast.8, bf16[80,1280]{1,0:T(8,128)(2,1)S(1)} %collective-permute-done.refs_1_, bf16[80,1280]{1,0:T(8,128)(2,1)S(1)} %collective-permute-done.1.refs_3_.refs_2_, bf16[80,1280]{1,0:T(8,128)(2,1)S(1)} %collective-permute-done.2.refs_0_.refs_3_, ...), custom_call_target="tpu_custom_call" | custom-call | flops 268435456 | bytes 1048576 | tf_op jit(solution)/shard_map/pallas_call | solution.py:31
  62.8 25.8 %all-to-all-done = bf16[64,8,2560]{2,1,0:T(8,128)(2,1)S(1)} async-done(((bf16[64,8,2560]{2,1,0:T(8,128)(2,1)}), bf16[64,8,2560]{2,1,0:T(8,128)(2,1)S(1)}, u32[]{:S(2)}, u32[]{:S(2)}) %all-to-all-start) | async-done | bytes 2621472 | tf_op jit(solution)/shard_map/all_to_all | solution.py:241
  88.6 0.0 copy-done.1
  88.6 0.0 copy-done.2
  88.6 7.6 %shard_map.77 = bf16[128,5120]{1,0:T(8,128)(2,1)} custom-call(bf16[1280,1280]{1,0:T(8,128)(2,1)} %shard_map.75.weight_in, bf16[512,2560]{1,0:T(8,128)(2,1)S(1)} %bitcast.4, f32[1280]{0:T(1024)S(1)} %copy-done.1, f32[1280]{0:T(1024)S(1)} %copy-done.2), custom_call_target="tpu_custom_call" | custom-call | flops 2147483648 | bytes 1048576 | tf_op jit(solution)/shard_map/pallas_call | solution.py:31
  (1 shorter events, 0.0 us)
Async XLA Ops:
  5.5 12.3 %copy-start = (bf16[1280,80]{0,1:T(8,128)(2,1)S(1)}, bf16[1280,80]{0,1:T(8,128)(2,1)}, u32[]{:S(2)}) copy-start(bf16[1280,80]{0,1:T(8,128)(2,1)} %param.11) | copy-start | bytes 614404
  5.5 83.2 %all-to-all-start = ((bf16[64,8,2560]{2,1,0:T(8,128)(2,1)}), bf16[64,8,2560]{2,1,0:T(8,128)(2,1)S(1)}, u32[]{:S(2)}, u32[]{:S(2)}) async-start(bf16[64,8,2560]{2,1,0:T(8,128)(2,1)} %bitcast.9), calls=%async_computation | async-start | bytes 5242880 | tf_op jit(solution)/shard_map/all_to_all | solution.py:241
  17.7 10.8 %collective-permute-start.3 = (bf16[80,1280]{1,0:T(8,128)(2,1)S(1)}, bf16[80,1280]{1,0:T(8,128)(2,1)S(1)}, u32[]{:S(2)}, u32[]{:S(2)}) collective-permute-start(bf16[80,1280]{1,0:T(8,128)(2,1)S(1)} %bitcast.5), channel_id=1, source_target_pairs={{0,128},{64,960},{128,256},{192,64},{256,384},{320,192},{384,512},... | collective-permute-start | bytes 614408 | tf_op jit(solution)/shard_map/ppermute | solution.py:203
  22.0 9.6 %collective-permute-start = (bf16[80,1280]{1,0:T(8,128)(2,1)S(1)}, bf16[80,1280]{1,0:T(8,128)(2,1)S(1)}, u32[]{:S(2)}, u32[]{:S(2)}) collective-permute-start(bf16[80,1280]{1,0:T(8,128)(2,1)S(1)} %bitcast.6), channel_id=1, source_target_pairs={{128,0},{960,64},{256,128},{64,192},{384,256},{192,320},{512,384},... | collective-permute-start | bytes 614408 | tf_op jit(solution)/shard_map/ppermute | solution.py:206
  28.6 10.4 %collective-permute-start.4 = (bf16[80,1280]{1,0:T(8,128)(2,1)S(1)}, bf16[80,1280]{1,0:T(8,128)(2,1)S(1)}, u32[]{:S(2)}, u32[]{:S(2)}) collective-permute-start(bf16[80,1280]{1,0:T(8,128)(2,1)S(1)} %collective-permute-done.3.refs_2_.refs_7_), channel_id=1, source_target_pairs={{0,128},{64,960},{128,256},{192,64},{256,384},{320,192},{384,512},... | collective-permute-start | bytes 614408 | tf_op jit(solution)/shard_map/ppermute | solution.py:203
  31.7 10.2 %collective-permute-start.1 = (bf16[80,1280]{1,0:T(8,128)(2,1)S(1)}, bf16[80,1280]{1,0:T(8,128)(2,1)S(1)}, u32[]{:S(2)}, u32[]{:S(2)}) collective-permute-start(bf16[80,1280]{1,0:T(8,128)(2,1)S(1)} %collective-permute-done.refs_1_), channel_id=1, source_target_pairs={{128,0},{960,64},{256,128},{64,192},{384,256},{192,320},{512,384},... | collective-permute-start | bytes 614408 | tf_op jit(solution)/shard_map/ppermute | solution.py:206
  39.0 9.1 %collective-permute-start.5 = (bf16[80,1280]{1,0:T(8,128)(2,1)S(1)}, bf16[80,1280]{1,0:T(8,128)(2,1)S(1)}, u32[]{:S(2)}, u32[]{:S(2)}) collective-permute-start(bf16[80,1280]{1,0:T(8,128)(2,1)S(1)} %collective-permute-done.4.refs_4_.refs_6_), channel_id=1, source_target_pairs={{0,128},{64,960},{128,256},{192,64},{256,384},{320,192},{384,512},... | collective-permute-start | bytes 614408 | tf_op jit(solution)/shard_map/ppermute | solution.py:203
  41.9 19.0 %collective-permute-start.7 = (bf16[5,80,1280]{2,1,0:T(8,128)(2,1)S(1)}, bf16[5,80,1280]{2,1,0:T(8,128)(2,1)S(1)}, u32[]{:S(2)}, u32[]{:S(2)}) collective-permute-start(bf16[5,80,1280]{2,1,0:T(8,128)(2,1)S(1)} %shard_map.73), channel_id=1, source_target_pairs={{0,64},{64,0},{128,192},{192,128},{256,320},{320,256},{384,448},{4... | collective-permute-start | bytes 3072008 | tf_op jit(solution)/shard_map/ppermute | solution.py:210
  43.8 7.9 %collective-permute-start.2 = (bf16[80,1280]{1,0:T(8,128)(2,1)S(1)}, bf16[80,1280]{1,0:T(8,128)(2,1)S(1)}, u32[]{:S(2)}, u32[]{:S(2)}) collective-permute-start(bf16[80,1280]{1,0:T(8,128)(2,1)S(1)} %collective-permute-done.1.refs_3_.refs_2_), channel_id=1, source_target_pairs={{128,0},{960,64},{256,128},{64,192},{384,256},{192,320},{512,384},... | collective-permute-start | bytes 614408 | tf_op jit(solution)/shard_map/ppermute | solution.py:206
  48.1 8.9 %collective-permute-start.6 = (bf16[80,1280]{1,0:T(8,128)(2,1)S(1)}, bf16[80,1280]{1,0:T(8,128)(2,1)S(1)}, u32[]{:S(2)}, u32[]{:S(2)}) collective-permute-start(bf16[80,1280]{1,0:T(8,128)(2,1)S(1)} %collective-permute-done.5.refs_1_.refs_5_), channel_id=1, source_target_pairs={{0,128},{64,960},{128,256},{192,64},{256,384},{320,192},{384,512},... | collective-permute-start | bytes 614408 | tf_op jit(solution)/shard_map/ppermute | solution.py:203
  57.0 31.7 %copy-start.1 = (f32[1280]{0:T(1024)S(1)}, f32[1280]{0:T(1024)}, u32[]{:S(2)}) copy-start(f32[1280]{0:T(1024)} %gain_ref.1) | copy-start | bytes 15364
  57.0 31.6 %copy-start.2 = (f32[1280]{0:T(1024)S(1)}, f32[1280]{0:T(1024)}, u32[]{:S(2)}) copy-start(f32[1280]{0:T(1024)} %bias_ref.1) | copy-start | bytes 15364
  57.0 3.9 %collective-permute-start.8 = (bf16[3,80,1280]{2,1,0:T(8,128)(2,1)S(1)}, bf16[3,80,1280]{2,1,0:T(8,128)(2,1)S(1)}, u32[]{:S(2)}, u32[]{:S(2)}) collective-permute-start(bf16[3,80,1280]{2,1,0:T(8,128)(2,1)S(1)} %shard_map.74), channel_id=1, source_target_pairs={{0,64},{64,0},{128,192},{192,128},{256,320},{320,256},{384,448},{4... | collective-permute-start | bytes 1843208 | tf_op jit(solution)/shard_map/ppermute | solution.py:210

commit v4 on v3

--- a/solution.py
+++ b/solution.py
@@ -81,7 +81,7 @@
     held = jnp.sum(jnp.where(hits, 1.0, 0.0), axis=1, keepdims=True)
     marker = jnp.where(held == 0.0, 64.0, 0.0)
     send_ref[:, :width] = (pick(hits, patch_ref[...]) + marker).astype(BF16)
-    leaves = [pltpu.make_async_copy(send_ref.at[:, :width], send_out.at[:, :width], left.at[4])]
+    leaves = [pltpu.make_async_copy(send_ref.at[:, :width], send_out.at[:, :width], left.at[2])]
     leaves[0].start()
     fetches[3].wait()
     lane, sub = iota((1, rows), 1), iota((rows, 1), 0)
@@ -105,13 +105,12 @@
         values = packed_ref[:, 2 * width + start : 2 * width + start + 256]
         mixed = jnp.dot(weights, values, preferred_element_type=F32).astype(BF16)
         context_ref[:, start : start + 256] = jnp.where(mine, mixed, context_ref[:, start : start + 256])
-    for i in range(4):
-        place = slice(i * lines // 4, (i + 1) * lines // 4)
-        wanted = iota((lines // 4, 1), 0) + i * lines // 4
+    for i in range(2):
+        place = slice(i * lines // 2, (i + 1) * lines // 2)
+        wanted = iota((lines // 2, 1), 0) + i * lines // 2
         send_ref[place, width:] = pick(key == wanted, context_ref[...]).astype(BF16)
-        leave = pltpu.make_async_copy(send_ref.at[place, width:], send_out.at[place, width:], left.at[i])
-        leave.start()
-        leaves.append(leave)
+        leaves.append(pltpu.make_async_copy(send_ref.at[place, width:], send_out.at[place, width:], left.at[i]))
+        leaves[-1].start()
     for leave in leaves:
         leave.wait()
 
@@ -160,7 +159,7 @@
         patches = received_ref[:, part].astype(F32)
         hidden_ref[:, part] = patches + project(received_ref[:, width:], weight_ref[part, :])
     leaves = []
-    chunk = min(256, lines)
+    chunk = min(128, lines)
     slots = chunk // 4
     row = iota((chunk, 1), 0)
     wanted = (row & (slots - 1)) * 4 + (row >> (slots.bit_length() - 1))
@@ -232,7 +231,7 @@
             pltpu.VMEM((rows, width), BF16),
             pltpu.VMEM((lines, 2 * width), BF16),
             pltpu.SemaphoreType.DMA((4,)),
-            pltpu.SemaphoreType.DMA((5,)),
+            pltpu.SemaphoreType.DMA((3,)),
         ],
         in_specs=[HBM] * 4,
         out_specs=HBM,

time: 96.7 us -> 96.5 us (level)
  the two profiles are of different devices: /device:TPU:638 before, /device:TPU:908 now
where the time goes in v4:
time: 96.5 us; the launch traced here: 96 us
  waiting for transfers between devices  42.5 us (44%)
  starting transfers between devices  38.5 us (40%)
  Pallas kernels  14.8 us (15%)
    all_to_all x1, waiting for transfers between devices, step(): lax.all_to_all(send, 'seq', split_axis=0, concat_axis=0, tiled=True)  29.1 us
    pallas_call x5, Pallas kernels, call(): pl.pallas_call(kernel, out_shape=out_shape, in_specs=in_specs or [SMEM] *...  14.8 us
    all_to_all x1, starting transfers between devices, step(): lax.all_to_all(send, 'seq', split_axis=0, concat_axis=0, tiled=True)  13.8 us
    ppermute x3, starting transfers between devices, ring_gather(): from_above = lax.ppermute(from_above, 'dp', down)  11.5 us
    ppermute x4, starting transfers between devices, ring_gather(): from_below = lax.ppermute(from_below, 'dp', up)  9.38 us
    ppermute x4, waiting for transfers between devices, ring_gather(): from_below = lax.ppermute(from_below, 'dp', up)  8.86 us
    ppermute x2, starting transfers between devices, ring_gather(): lax.ppermute(pack([blocks[j] for j in part]), 'dp', swap)  3.84 us
    ppermute x3, waiting for transfers between devices, ring_gather(): from_above = lax.ppermute(from_above, 'dp', down)  2.51 us
  transfers between devices with their start and end apart: 10, of which 6 were waited for; matrix products, arithmetic and copies ran while one was open for 0% of the time, Pallas kernels for 2%

profile of v4, /device:TPU:908, one launch (start us, length us, event | category | flops | bytes accessed | tf_op | source)
XLA Modules:
  0.0 96.0 jit_solution(10690820607113527714)
XLA Ops:
  0.0 5.5 %shard_map.76 = bf16[512,2560]{1,0:T(8,128)(2,1)} custom-call(s32[1,4]{1,0:T(1,128)} %counts_in.1, s32[1,48]{1,0:T(1,128)} %bitcast.10, bf16[192,3840]{1,0:T(8,128)(2,1)} %packed_in.1, bf16[192,1280]{1,0:T(8,128)(2,1)} %patch_in.1), custom_call_target="tpu_custom_call" | custom-call | flops 2147483648 | bytes 1048576 | tf_op jit(solution)/shard_map/pallas_call | solution.py:31
  5.5 0.0 copy-start
  5.5 13.8 %all-to-all-start = ((bf16[64,8,2560]{2,1,0:T(8,128)(2,1)}), bf16[64,8,2560]{2,1,0:T(8,128)(2,1)S(1)}, u32[]{:S(2)}, u32[]{:S(2)}) async-start(bf16[64,8,2560]{2,1,0:T(8,128)(2,1)} %bitcast.9), calls=%async_computation | async-start | bytes 5242880 | tf_op jit(solution)/shard_map/all_to_all | solution.py:240
  19.3 0.0 copy-done
  19.3 1.9 %collective-permute-start.3 = (bf16[80,1280]{1,0:T(8,128)(2,1)S(1)}, bf16[80,1280]{1,0:T(8,128)(2,1)S(1)}, u32[]{:S(2)}, u32[]{:S(2)}) collective-permute-start(bf16[80,1280]{1,0:T(8,128)(2,1)S(1)} %bitcast.5), channel_id=1, source_target_pairs={{0,128},{64,960},{128,256},{192,64},{256,384},{320,192},{384,512},... | collective-permute-start | bytes 614408 | tf_op jit(solution)/shard_map/ppermute | solution.py:202
  21.2 3.9 %collective-permute-start = (bf16[80,1280]{1,0:T(8,128)(2,1)S(1)}, bf16[80,1280]{1,0:T(8,128)(2,1)S(1)}, u32[]{:S(2)}, u32[]{:S(2)}) collective-permute-start(bf16[80,1280]{1,0:T(8,128)(2,1)S(1)} %bitcast.6), channel_id=1, source_target_pairs={{128,0},{960,64},{256,128},{64,192},{384,256},{192,320},{512,384},... | collective-permute-start | bytes 614408 | tf_op jit(solution)/shard_map/ppermute | solution.py:205
  25.1 3.8 %collective-permute-done.3.refs_2_.refs_7_ = bf16[80,1280]{1,0:T(8,128)(2,1)S(1)} collective-permute-done((bf16[80,1280]{1,0:T(8,128)(2,1)S(1)}, bf16[80,1280]{1,0:T(8,128)(2,1)S(1)}, u32[]{:S(2)}, u32[]{:S(2)}) %collective-permute-start.3) | collective-permute-done | bytes 204832 | tf_op jit(solution)/shard_map/ppermute | solution.py:202
  28.9 1.9 %collective-permute-start.4 = (bf16[80,1280]{1,0:T(8,128)(2,1)S(1)}, bf16[80,1280]{1,0:T(8,128)(2,1)S(1)}, u32[]{:S(2)}, u32[]{:S(2)}) collective-permute-start(bf16[80,1280]{1,0:T(8,128)(2,1)S(1)} %collective-permute-done.3.refs_2_.refs_7_), channel_id=1, source_target_pairs={{0,128},{64,960},{128,256},{192,64},{256,384},{320,192},{384,512},... | collective-permute-start | bytes 614408 | tf_op jit(solution)/shard_map/ppermute | solution.py:202
  30.8 0.0 collective-permute-done.refs_1_
  30.8 3.9 %collective-permute-start.1 = (bf16[80,1280]{1,0:T(8,128)(2,1)S(1)}, bf16[80,1280]{1,0:T(8,128)(2,1)S(1)}, u32[]{:S(2)}, u32[]{:S(2)}) collective-permute-start(bf16[80,1280]{1,0:T(8,128)(2,1)S(1)} %collective-permute-done.refs_1_), channel_id=1, source_target_pairs={{128,0},{960,64},{256,128},{64,192},{384,256},{192,320},{512,384},... | collective-permute-start | bytes 614408 | tf_op jit(solution)/shard_map/ppermute | solution.py:205
  34.7 3.4 %collective-permute-done.4.refs_4_.refs_6_ = bf16[80,1280]{1,0:T(8,128)(2,1)S(1)} collective-permute-done((bf16[80,1280]{1,0:T(8,128)(2,1)S(1)}, bf16[80,1280]{1,0:T(8,128)(2,1)S(1)}, u32[]{:S(2)}, u32[]{:S(2)}) %collective-permute-start.4) | collective-permute-done | bytes 204832 | tf_op jit(solution)/shard_map/ppermute | solution.py:202
  38.1 2.2 %collective-permute-start.5 = (bf16[80,1280]{1,0:T(8,128)(2,1)S(1)}, bf16[80,1280]{1,0:T(8,128)(2,1)S(1)}, u32[]{:S(2)}, u32[]{:S(2)}) collective-permute-start(bf16[80,1280]{1,0:T(8,128)(2,1)S(1)} %collective-permute-done.4.refs_4_.refs_6_), channel_id=1, source_target_pairs={{0,128},{64,960},{128,256},{192,64},{256,384},{320,192},{384,512},... | collective-permute-start | bytes 614408 | tf_op jit(solution)/shard_map/ppermute | solution.py:202
  40.3 0.0 collective-permute-done.1.refs_3_.refs_2_
  40.3 0.1 shard_map.73
  40.4 1.9 %collective-permute-start.7 = (bf16[5,80,1280]{2,1,0:T(8,128)(2,1)S(1)}, bf16[5,80,1280]{2,1,0:T(8,128)(2,1)S(1)}, u32[]{:S(2)}, u32[]{:S(2)}) collective-permute-start(bf16[5,80,1280]{2,1,0:T(8,128)(2,1)S(1)} %shard_map.73), channel_id=1, source_target_pairs={{0,64},{64,0},{128,192},{192,128},{256,320},{320,256},{384,448},{4... | collective-permute-start | bytes 3072008 | tf_op jit(solution)/shard_map/ppermute | solution.py:209
  42.3 3.7 %collective-permute-start.2 = (bf16[80,1280]{1,0:T(8,128)(2,1)S(1)}, bf16[80,1280]{1,0:T(8,128)(2,1)S(1)}, u32[]{:S(2)}, u32[]{:S(2)}) collective-permute-start(bf16[80,1280]{1,0:T(8,128)(2,1)S(1)} %collective-permute-done.1.refs_3_.refs_2_), channel_id=1, source_target_pairs={{128,0},{960,64},{256,128},{64,192},{384,256},{192,320},{512,384},... | collective-permute-start | bytes 614408 | tf_op jit(solution)/shard_map/ppermute | solution.py:205
  46.0 0.0 collective-permute-done.5.refs_1_.refs_5_
  46.0 3.4 %collective-permute-start.6 = (bf16[80,1280]{1,0:T(8,128)(2,1)S(1)}, bf16[80,1280]{1,0:T(8,128)(2,1)S(1)}, u32[]{:S(2)}, u32[]{:S(2)}) collective-permute-start(bf16[80,1280]{1,0:T(8,128)(2,1)S(1)} %collective-permute-done.5.refs_1_.refs_5_), channel_id=1, source_target_pairs={{0,128},{64,960},{128,256},{192,64},{256,384},{320,192},{384,512},... | collective-permute-start | bytes 614408 | tf_op jit(solution)/shard_map/ppermute | solution.py:202
  49.4 2.5 %collective-permute-done.2.refs_0_.refs_3_ = bf16[80,1280]{1,0:T(8,128)(2,1)S(1)} collective-permute-done((bf16[80,1280]{1,0:T(8,128)(2,1)S(1)}, bf16[80,1280]{1,0:T(8,128)(2,1)S(1)}, u32[]{:S(2)}, u32[]{:S(2)}) %collective-permute-start.2) | collective-permute-done | bytes 204832 | tf_op jit(solution)/shard_map/ppermute | solution.py:205
  51.9 1.8 %collective-permute-done.6.refs_2_.refs_4_ = bf16[80,1280]{1,0:T(8,128)(2,1)S(1)} collective-permute-done((bf16[80,1280]{1,0:T(8,128)(2,1)S(1)}, bf16[80,1280]{1,0:T(8,128)(2,1)S(1)}, u32[]{:S(2)}, u32[]{:S(2)}) %collective-permute-start.6) | collective-permute-done | bytes 204832 | tf_op jit(solution)/shard_map/ppermute | solution.py:202
  53.7 0.0 copy-start.1
  53.7 0.0 copy-start.2
  53.7 1.9 %collective-permute-start.8 = (bf16[3,80,1280]{2,1,0:T(8,128)(2,1)S(1)}, bf16[3,80,1280]{2,1,0:T(8,128)(2,1)S(1)}, u32[]{:S(2)}, u32[]{:S(2)}) collective-permute-start(bf16[3,80,1280]{2,1,0:T(8,128)(2,1)S(1)} %shard_map.74), channel_id=1, source_target_pairs={{0,64},{64,0},{128,192},{192,128},{256,320},{320,256},{384,448},{4... | collective-permute-start | bytes 1843208 | tf_op jit(solution)/shard_map/ppermute | solution.py:209
  55.6 2.0 %collective-permute-done.8.refs_9_ = bf16[3,80,1280]{2,1,0:T(8,128)(2,1)S(1)} collective-permute-done((bf16[3,80,1280]{2,1,0:T(8,128)(2,1)S(1)}, bf16[3,80,1280]{2,1,0:T(8,128)(2,1)S(1)}, u32[]{:S(2)}, u32[]{:S(2)}) %collective-permute-start.8) | collective-permute-done | bytes 614432 | tf_op jit(solution)/shard_map/ppermute | solution.py:209
  57.6 0.0 collective-permute-done.7.refs_8_
  57.6 1.9 %shard_map.75.weight_in = bf16[1280,1280]{1,0:T(8,128)(2,1)} custom-call(bf16[80,1280]{1,0:T(8,128)(2,1)S(1)} %bitcast.8, bf16[80,1280]{1,0:T(8,128)(2,1)S(1)} %collective-permute-done.refs_1_, bf16[80,1280]{1,0:T(8,128)(2,1)S(1)} %collective-permute-done.1.refs_3_.refs_2_, bf16[80,1280]{1,0:T(8,128)(2,1)S(1)} %collective-permute-done.2.refs_0_.refs_3_, ...), custom_call_target="tpu_custom_call" | custom-call | flops 268435456 | bytes 1048576 | tf_op jit(solution)/shard_map/pallas_call | solution.py:31
  59.5 29.1 %all-to-all-done = bf16[64,8,2560]{2,1,0:T(8,128)(2,1)S(1)} async-done(((bf16[64,8,2560]{2,1,0:T(8,128)(2,1)}), bf16[64,8,2560]{2,1,0:T(8,128)(2,1)S(1)}, u32[]{:S(2)}, u32[]{:S(2)}) %all-to-all-start) | async-done | bytes 2621472 | tf_op jit(solution)/shard_map/all_to_all | solution.py:240
  88.6 0.0 copy-done.1
  88.6 0.0 copy-done.2
  88.7 7.4 %shard_map.77 = bf16[128,5120]{1,0:T(8,128)(2,1)} custom-call(bf16[1280,1280]{1,0:T(8,128)(2,1)} %shard_map.75.weight_in, bf16[512,2560]{1,0:T(8,128)(2,1)S(1)} %bitcast.4, f32[1280]{0:T(1024)S(1)} %copy-done.1, f32[1280]{0:T(1024)S(1)} %copy-done.2), custom_call_target="tpu_custom_call" | custom-call | flops 2147483648 | bytes 1048576 | tf_op jit(solution)/shard_map/pallas_call | solution.py:31
  (1 shorter events, 0.0 us)
Async XLA Ops:
  5.5 13.8 %copy-start = (bf16[1280,80]{0,1:T(8,128)(2,1)S(1)}, bf16[1280,80]{0,1:T(8,128)(2,1)}, u32[]{:S(2)}) copy-start(bf16[1280,80]{0,1:T(8,128)(2,1)} %param.11) | copy-start | bytes 614404
  5.5 83.2 %all-to-all-start = ((bf16[64,8,2560]{2,1,0:T(8,128)(2,1)}), bf16[64,8,2560]{2,1,0:T(8,128)(2,1)S(1)}, u32[]{:S(2)}, u32[]{:S(2)}) async-start(bf16[64,8,2560]{2,1,0:T(8,128)(2,1)} %bitcast.9), calls=%async_computation | async-start | bytes 5242880 | tf_op jit(solution)/shard_map/all_to_all | solution.py:240
  19.3 9.6 %collective-permute-start.3 = (bf16[80,1280]{1,0:T(8,128)(2,1)S(1)}, bf16[80,1280]{1,0:T(8,128)(2,1)S(1)}, u32[]{:S(2)}, u32[]{:S(2)}) collective-permute-start(bf16[80,1280]{1,0:T(8,128)(2,1)S(1)} %bitcast.5), channel_id=1, source_target_pairs={{0,128},{64,960},{128,256},{192,64},{256,384},{320,192},{384,512},... | collective-permute-start | bytes 614408 | tf_op jit(solution)/shard_map/ppermute | solution.py:202
  21.2 9.6 %collective-permute-start = (bf16[80,1280]{1,0:T(8,128)(2,1)S(1)}, bf16[80,1280]{1,0:T(8,128)(2,1)S(1)}, u32[]{:S(2)}, u32[]{:S(2)}) collective-permute-start(bf16[80,1280]{1,0:T(8,128)(2,1)S(1)} %bitcast.6), channel_id=1, source_target_pairs={{128,0},{960,64},{256,128},{64,192},{384,256},{192,320},{512,384},... | collective-permute-start | bytes 614408 | tf_op jit(solution)/shard_map/ppermute | solution.py:205
  28.9 9.2 %collective-permute-start.4 = (bf16[80,1280]{1,0:T(8,128)(2,1)S(1)}, bf16[80,1280]{1,0:T(8,128)(2,1)S(1)}, u32[]{:S(2)}, u32[]{:S(2)}) collective-permute-start(bf16[80,1280]{1,0:T(8,128)(2,1)S(1)} %collective-permute-done.3.refs_2_.refs_7_), channel_id=1, source_target_pairs={{0,128},{64,960},{128,256},{192,64},{256,384},{320,192},{384,512},... | collective-permute-start | bytes 614408 | tf_op jit(solution)/shard_map/ppermute | solution.py:202
  30.8 9.5 %collective-permute-start.1 = (bf16[80,1280]{1,0:T(8,128)(2,1)S(1)}, bf16[80,1280]{1,0:T(8,128)(2,1)S(1)}, u32[]{:S(2)}, u32[]{:S(2)}) collective-permute-start(bf16[80,1280]{1,0:T(8,128)(2,1)S(1)} %collective-permute-done.refs_1_), channel_id=1, source_target_pairs={{128,0},{960,64},{256,128},{64,192},{384,256},{192,320},{512,384},... | collective-permute-start | bytes 614408 | tf_op jit(solution)/shard_map/ppermute | solution.py:205
  38.1 7.9 %collective-permute-start.5 = (bf16[80,1280]{1,0:T(8,128)(2,1)S(1)}, bf16[80,1280]{1,0:T(8,128)(2,1)S(1)}, u32[]{:S(2)}, u32[]{:S(2)}) collective-permute-start(bf16[80,1280]{1,0:T(8,128)(2,1)S(1)} %collective-permute-done.4.refs_4_.refs_6_), channel_id=1, source_target_pairs={{0,128},{64,960},{128,256},{192,64},{256,384},{320,192},{384,512},... | collective-permute-start | bytes 614408 | tf_op jit(solution)/shard_map/ppermute | solution.py:202
  40.4 17.3 %collective-permute-start.7 = (bf16[5,80,1280]{2,1,0:T(8,128)(2,1)S(1)}, bf16[5,80,1280]{2,1,0:T(8,128)(2,1)S(1)}, u32[]{:S(2)}, u32[]{:S(2)}) collective-permute-start(bf16[5,80,1280]{2,1,0:T(8,128)(2,1)S(1)} %shard_map.73), channel_id=1, source_target_pairs={{0,64},{64,0},{128,192},{192,128},{256,320},{320,256},{384,448},{4... | collective-permute-start | bytes 3072008 | tf_op jit(solution)/shard_map/ppermute | solution.py:209
  42.3 9.6 %collective-permute-start.2 = (bf16[80,1280]{1,0:T(8,128)(2,1)S(1)}, bf16[80,1280]{1,0:T(8,128)(2,1)S(1)}, u32[]{:S(2)}, u32[]{:S(2)}) collective-permute-start(bf16[80,1280]{1,0:T(8,128)(2,1)S(1)} %collective-permute-done.1.refs_3_.refs_2_), channel_id=1, source_target_pairs={{128,0},{960,64},{256,128},{64,192},{384,256},{192,320},{512,384},... | collective-permute-start | bytes 614408 | tf_op jit(solution)/shard_map/ppermute | solution.py:205
  46.0 7.7 %collective-permute-start.6 = (bf16[80,1280]{1,0:T(8,128)(2,1)S(1)}, bf16[80,1280]{1,0:T(8,128)(2,1)S(1)}, u32[]{:S(2)}, u32[]{:S(2)}) collective-permute-start(bf16[80,1280]{1,0:T(8,128)(2,1)S(1)} %collective-permute-done.5.refs_1_.refs_5_), channel_id=1, source_target_pairs={{0,128},{64,960},{128,256},{192,64},{256,384},{320,192},{384,512},... | collective-permute-start | bytes 614408 | tf_op jit(solution)/shard_map/ppermute | solution.py:202
  53.7 35.0 %copy-start.1 = (f32[1280]{0:T(1024)S(1)}, f32[1280]{0:T(1024)}, u32[]{:S(2)}) copy-start(f32[1280]{0:T(1024)} %gain_ref.1) | copy-start | bytes 15364
  53.7 35.0 %copy-start.2 = (f32[1280]{0:T(1024)S(1)}, f32[1280]{0:T(1024)}, u32[]{:S(2)}) copy-start(f32[1280]{0:T(1024)} %bias_ref.1) | copy-start | bytes 15364
  53.7 3.9 %collective-permute-start.8 = (bf16[3,80,1280]{2,1,0:T(8,128)(2,1)S(1)}, bf16[3,80,1280]{2,1,0:T(8,128)(2,1)S(1)}, u32[]{:S(2)}, u32[]{:S(2)}) collective-permute-start(bf16[3,80,1280]{2,1,0:T(8,128)(2,1)S(1)} %shard_map.74), channel_id=1, source_target_pairs={{0,64},{64,0},{128,192},{192,128},{256,320},{320,256},{384,448},{4... | collective-permute-start | bytes 1843208 | tf_op jit(solution)/shard_map/ppermute | solution.py:209
